TPU v7x, 128 devices: a whole 4x4x4 slice. The times are simulated.
128 devices in a mesh: dp: 32 (over y, x, core), tp: 4 (over z).
Axes of the slice: x: 4, y: 4, z: 4, core: 2. Of those that a mesh axis runs over, the one named last changes fastest.
Arguments:
- tokens: bfloat16 [16384, 4096], P(('dp', 'tp')), may hold values from -6 to 6
- norm_gain: float32 [4096], replicated, may hold values from 0.1 to 1.9
- w_query: bfloat16 [4096, 4096], P(None, 'tp'), may hold values from -0.09375 to 0.09375
- w_key: bfloat16 [4096, 1024], P(None, 'tp'), may hold values from -2.34375 to 2.34375
- w_value: bfloat16 [4096, 1024], P(None, 'tp'), may hold values from -0.09375 to 0.09375
- w_output: bfloat16 [4096, 4096], P('tp'), may hold values from -0.09375 to 0.09375
- doc_lengths: int32 [128], replicated, may hold values from 1 to 512, as said below
- pack_index: int32 [16384], replicated, may hold values from 0 to 16383, as said below
Outputs:
- output: bfloat16 [16384, 4096], P(('dp', 'tp'))
Inputs may be any that keep to these rules, and one draw needn't show every extreme that they name: `doc_lengths`: each run of 4 documents numbered g * 4 to g * 4 + 4 - 1 (the documents of group g) holds at most 1024 tokens together, and some group holds exactly 1024. No document is longer than 512 tokens, and one has exactly that many. `pack_index`: each packed position appears once. The 128 rows of one device hold at most 8 tokens of the documents of any one group; every device holds the same number of one group's tokens, up to one.
All inputs are finite; a program needn't handle non-finite values.
Results may differ from a plain program's by a relative error of at most 0.01.
Values may be sent and summed in bfloat16 or wider, within the bound.
A program may use at most 128 MiB of HBM per device.

v0:
```python
import jax
import jax.numpy as jnp
from jax import lax
from jax.sharding import PartitionSpec as P

HEAD_DIM = 128
GROUP_DOCS = 4


rope_base = 500000.0
norm_eps = 1e-05
score_floor = -1e30


def split_up(array, dim, length):
    dims = array.shape
    pieces = array.reshape(*dims[:dim], length, dims[dim] // length, *dims[dim + 1 :])
    return jnp.moveaxis(pieces, dim, 0)


def sum_at_owner(array, axis, dim):
    pieces = split_up(array, dim, lax.axis_size(axis))
    arrived = lax.all_to_all(pieces, axis, split_axis=0, concat_axis=0, tiled=True)
    return arrived.astype(jnp.float32).sum(axis=0)


def row_tables(pack_index, doc_lengths, group_count, tok_dev):
    doc_ends = jnp.cumsum(doc_lengths)
    doc_starts = doc_ends - doc_lengths
    inside = (
        (pack_index[:, None] >= doc_starts[None, :]) & (pack_index[:, None] < doc_ends[None, :])
    ).astype(jnp.int32)
    doc_index = jnp.sum(inside * jnp.arange(doc_lengths.shape[0], dtype=jnp.int32)[None, :], axis=1)
    position = pack_index - jnp.sum(inside * doc_starts[None, :], axis=1)
    owner_group = doc_index // GROUP_DOCS
    member = (
        owner_group.reshape(-1, tok_dev)[:, :, None]
        == jnp.arange(group_count, dtype=jnp.int32)[None, None, :]
    ).astype(jnp.int32)
    slot_rank = jnp.sum((jnp.cumsum(member, axis=1) - 1) * member, axis=2)
    return (doc_index, position, owner_group, slot_rank.reshape(-1))


def rotate(projected, position, head_count):
    row_count = projected.shape[0]
    half_dim = HEAD_DIM // 2
    spread = projected.reshape(row_count, head_count, HEAD_DIM)
    frequency = rope_base ** (-2.0 * jnp.arange(half_dim, dtype=jnp.float32) / HEAD_DIM)
    angles = position.astype(jnp.float32)[:, None] * frequency[None, :]
    cosine = jnp.cos(angles)[:, None, :]
    sine = jnp.sin(angles)[:, None, :]
    lower_part = spread[:, :, :half_dim]
    upper_part = spread[:, :, half_dim:]
    turned = jnp.concatenate(
        [lower_part * cosine - upper_part * sine, upper_part * cosine + lower_part * sine], axis=2
    )
    return turned.reshape(row_count, head_count * HEAD_DIM)


def attend(query, key_rows, value_rows, segment, places, head_count, kv_count):
    slot_total = query.shape[0]
    group_size = head_count // kv_count
    score_scale = HEAD_DIM ** (-0.5)
    block_rows = min(512, slot_total)
    query_heads = query.reshape(slot_total, kv_count, group_size, HEAD_DIM)
    key_heads = key_rows.reshape(slot_total, kv_count, HEAD_DIM)
    value_heads = value_rows.reshape(slot_total, kv_count, HEAD_DIM)
    outputs = []
    for block_start in range(0, slot_total, block_rows):
        query_block = query_heads[block_start : block_start + block_rows]
        score_values = (
            jnp.einsum("qkgd,skd->kgqs", query_block, key_heads, preferred_element_type=jnp.float32)
            * score_scale
        )
        block_segment = segment[block_start : block_start + block_rows]
        block_places = places[block_start : block_start + block_rows]
        allowed = (block_segment[:, None] == segment[None, :]) & (
            places[None, :] <= block_places[:, None]
        )
        score_values = jnp.where(allowed[None, None], score_values, score_floor)
        row_peak = jnp.max(score_values, axis=-1, keepdims=True)
        weights = jnp.exp(score_values - row_peak)
        weights = (weights / jnp.sum(weights, axis=-1, keepdims=True)).astype(jnp.bfloat16)
        mixed_values = jnp.einsum(
            "kgqs,skd->qkgd", weights, value_heads, preferred_element_type=jnp.float32
        )
        outputs.append(mixed_values.astype(jnp.bfloat16).reshape(block_rows, head_count * HEAD_DIM))
    return jnp.concatenate(outputs, axis=0)


def body(tokens, norm_gain, w_query, w_key, w_value, w_output, doc_lengths, pack_index):
    group_count = lax.axis_size("dp")
    tp_count = lax.axis_size("tp")
    tok_dev = tokens.shape[0]
    model_width = tokens.shape[1]
    send_slots = 2 * tok_dev // group_count
    device_total = group_count * tp_count
    slot_total = device_total * send_slots
    group_rows = group_count * send_slots
    my_group = lax.axis_index("dp")
    my_source = my_group * tp_count + lax.axis_index("tp")
    doc_index, position, owner_group, slot_rank = row_tables(
        pack_index, doc_lengths, group_count, tok_dev
    )
    own_group = lax.dynamic_slice_in_dim(owner_group, my_source * tok_dev, tok_dev)
    own_rank = lax.dynamic_slice_in_dim(slot_rank, my_source * tok_dev, tok_dev)
    send_index = own_group * send_slots + own_rank
    residual = tokens.astype(jnp.float32)
    normed = (
        residual
        * lax.rsqrt(jnp.mean(residual * residual, axis=1, keepdims=True) + norm_eps)
        * norm_gain
    ).astype(jnp.bfloat16)
    outgoing = jnp.zeros((group_rows, model_width), jnp.bfloat16).at[send_index].set(normed)
    fanned = jnp.broadcast_to(
        outgoing.reshape(group_count, 1, send_slots, model_width),
        (group_count, tp_count, send_slots, model_width),
    )
    arrived = lax.all_to_all(
        fanned.reshape(slot_total, model_width),
        ("dp", "tp"),
        split_axis=0,
        concat_axis=0,
        tiled=True,
    )
    mine = (owner_group == my_group).reshape(device_total, tok_dev)
    slot_match = (
        slot_rank.reshape(device_total, tok_dev)[:, :, None]
        == jnp.arange(send_slots, dtype=jnp.int32)[None, None, :]
    )
    pick = (mine[:, :, None] & slot_match).astype(jnp.int32)
    occupied = jnp.sum(pick, axis=1).reshape(slot_total)
    slot_doc = jnp.sum(pick * doc_index.reshape(device_total, tok_dev, 1), axis=1).reshape(
        slot_total
    )
    slot_place = jnp.sum(pick * position.reshape(device_total, tok_dev, 1), axis=1).reshape(
        slot_total
    )
    segment = jnp.where(occupied > 0, slot_doc, -1 - jnp.arange(slot_total, dtype=jnp.int32))
    head_count = w_query.shape[1] // HEAD_DIM
    kv_count = w_key.shape[1] // HEAD_DIM
    query = rotate(
        jnp.dot(arrived, w_query, preferred_element_type=jnp.float32), slot_place, head_count
    ).astype(jnp.bfloat16)
    key_rows = rotate(
        jnp.dot(arrived, w_key, preferred_element_type=jnp.float32), slot_place, kv_count
    ).astype(jnp.bfloat16)
    value_rows = jnp.dot(arrived, w_value, preferred_element_type=jnp.float32).astype(jnp.bfloat16)
    context = attend(query, key_rows, value_rows, segment, slot_place, head_count, kv_count)
    came_back = lax.all_to_all(context, "dp", split_axis=0, concat_axis=0, tiled=True)
    group_span = tp_count * tok_dev
    group_owner = lax.dynamic_slice_in_dim(owner_group, my_group * group_span, group_span)
    group_rank = lax.dynamic_slice_in_dim(slot_rank, my_group * group_span, group_span)
    source_member = jnp.arange(group_span, dtype=jnp.int32) // tok_dev
    fetch_index = group_owner * (tp_count * send_slots) + source_member * send_slots + group_rank
    compact = jnp.take(came_back, fetch_index, axis=0)
    attended = sum_at_owner(
        jnp.dot(compact, w_output, preferred_element_type=jnp.float32).astype(jnp.bfloat16), "tp", 0
    )
    return (residual + attended).astype(jnp.bfloat16)


def solution(mesh):
    placed = (
        P(("dp", "tp"), None),
        P(),
        P(None, "tp"),
        P(None, "tp"),
        P(None, "tp"),
        P("tp", None),
        P(),
        P(),
    )
    return jax.shard_map(
        body, mesh=mesh, in_specs=placed, out_specs=P(("dp", "tp"), None), check_vma=False
    )
```

profile of v0, /device:TPU:0, one launch (start us, length us, event | category | flops | bytes accessed | tf_op | source)
XLA Modules:
  0.0 300.7 jit_solution(13517198028188437393)
XLA Ops:
  1.9 8.0 %select_reduce_fusion = (s32[16384]{0:T(1024)S(1)}, s32[16384]{0:T(1024)S(1)}) fusion(s32[128]{0:T(128)S(1)} %reduce, s32[128]{0:T(128)S(1)} %sub.56, s32[16384]{0:T(1024)} %param.15), kind=kLoop, calls=%fused_computation.23 | loop fusion | flops 14647296 | bytes 197632 | tf_op jit(solution)/shard_map/reduce_sum | solution.py:34
  11.1 1.5 fusion.18
  12.7 4.5 %scatter_custom_fusion = bf16[256,4096]{1,0:T(8,128)(2,1)} fusion(s32[128]{0:T(128)S(1)} %compare_select_fusion.1, bf16[128,4096]{1,0:T(8,128)(2,1)} %param.8, f32[4096]{0:T(1024)} %param.9, f32[128]{0:T(128)S(1)} %add_rsqrt_fusion, bf16[]{:T(256)} %constant.93.clone.1), kind=kCustom, calls=%fused_computation.55 | custom fusion | flops 2097152 | bytes 3162626 | tf_op jit(solution)/shard_map/scatter | solution.py:114
  17.3 5.9 %broadcast_in_dim.39 = bf16[32,4,8,4096]{3,2,1,0:T(8,128)(2,1)} broadcast(bf16[32,8,4096]{2,1,0:T(8,128)(2,1)} %bitcast.96), dimensions={0,2,3} | broadcast | bytes 10485760 | tf_op jit(solution)/shard_map/broadcast_in_dim | solution.py:115
  23.1 11.9 %all-to-all-start = ((bf16[128,8,4096]{2,1,0:T(8,128)(2,1)}), bf16[128,8,4096]{2,1,0:T(8,128)(2,1)}, u32[]{:S(2)}, u32[]{:S(2)}) async-start(bf16[128,8,4096]{2,1,0:T(8,128)(2,1)} %bitcast.95), calls=%async_computation | async-start | bytes 16777216 | tf_op jit(solution)/shard_map/all_to_all | solution.py:119
  35.1 6.5 %select_reduce_fusion.4 = (s32[128,8]{1,0:T(8,128)S(1)}, s32[128,8]{1,0:T(8,128)S(1)}, s32[128,8]{1,0:T(8,128)S(1)}) fusion(s32[128,128]{1,0:T(8,128)S(1)} %bitcast.103, s32[128,128]{1,0:T(8,128)S(1)} %copy.62, pred[128,128]{1,0:T(8,128)(4,1)S(1)} %broadcast_compare_fusion.1, s32[128,128]{1,0:T(8,128)S(1)} %subtract_bitcast_fusion), kind=kLoop, calls=%fused_computation.68 | loop fusion | flops 1045504 | bytes 225280 | tf_op jit(solution)/shard_map/reduce_sum | solution.py:133
  42.2 11.5 %copy.84 = bf16[1024,4096]{1,0:T(8,128)(2,1)} copy(bf16[1024,4096]{0,1:T(8,128)(2,1)} %bitcast.97) | data formatting | bytes 16777216 | tf_op jit(solution)/shard_map/dot_general | solution.py:143
  53.7 4.1 %copy.81 = bf16[256,4096]{1,0:T(8,128)(2,1)} copy(bf16[256,4096]{0,1:T(8,128)(2,1)} %bitcast.101) | data formatting | bytes 4194304 | tf_op jit(solution)/shard_map/dot_general | solution.py:146
  58.8 2.0 compare_and_fusion.2
  60.8 74.4 %all-to-all-done = bf16[128,8,4096]{2,1,0:T(8,128)(2,1)} async-done(((bf16[128,8,4096]{2,1,0:T(8,128)(2,1)}), bf16[128,8,4096]{2,1,0:T(8,128)(2,1)}, u32[]{:S(2)}, u32[]{:S(2)}) %all-to-all-start) | async-done | bytes 8388640 | tf_op jit(solution)/shard_map/all_to_all | solution.py:119
  135.2 12.9 %fusion.4 = f32[1024,8,128]{0,2,1:T(8,128)S(1)} fusion(bf16[8,128,4096]{2,1,0:T(8,128)(2,1)} %bitcast.98, bf16[128,8,4096]{2,1,0:T(8,128)(2,1)} %all-to-all-done), kind=kOutput, calls=%fused_computation.12 | convolution fusion | flops 8589934592 | bytes 20971520 | tf_op jit(solution)/shard_map/dot_general | solution.py:143
  149.7 5.7 %fusion.6 = f32[1024,2,128]{0,2,1:T(8,128)S(1)} fusion(bf16[2,128,4096]{2,1,0:T(8,128)(2,1)S(1)} %bitcast.102, bf16[128,8,4096]{2,1,0:T(8,128)(2,1)} %all-to-all-done), kind=kOutput, calls=%fused_computation.14 | convolution fusion | flops 2147483648 | bytes 11534336 | tf_op jit(solution)/shard_map/dot_general | solution.py:146
  157.5 11.1 %fusion.61 = (f32[2,4,512]{2,1,0:T(4,128)S(1)}, f32[2,4,512,1024]{2,3,1,0:T(8,128)}) fusion(pred[512,1024]{0,1:T(8,128)(4,1)} %get-tuple-element.21, bf16[512,2,4,128]{0,3,2,1:T(8,128)(2,1)} %bitcast.107, bf16[1024,2,64]{0,2,1:T(8,128)(2,1)} %get-tuple-element.17, bf16[1024,2,64]{0,2,1:T(8,128)(2,1)S(1)} %get-tuple-element.16), kind=kOutput, calls=%fused_computation.115 | convolution fusion | flops 1091568640 | bytes 18890752 | tf_op jit(solution)/shard_map/sub | solution.py:82
  168.6 5.9 %fusion.30 = bf16[1024,256]{0,1:T(8,128)(2,1)S(1)} fusion(bf16[4096,256]{1,0:T(8,128)(2,1)S(1)} %copy-done, bf16[128,8,4096]{2,1,0:T(8,128)(2,1)} %all-to-all-done), kind=kOutput, calls=%fused_computation.53 | convolution fusion | flops 2147745792 | bytes 11010048 | tf_op jit(solution)/shard_map/dot_general | solution.py:148
  174.6 2.4 copy-done.7
  177.0 1.5 fusion.28
  179.1 11.2 %fusion.62 = (f32[2,4,512]{2,1,0:T(4,128)S(1)}, f32[2,4,512,1024]{2,3,1,0:T(8,128)}) fusion(pred[512,1024]{0,1:T(8,128)(4,1)} %get-tuple-element.20, bf16[512,2,4,128]{0,3,2,1:T(8,128)(2,1)S(1)} %bitcast.106, bf16[1024,2,64]{0,2,1:T(8,128)(2,1)} %get-tuple-element.17, bf16[1024,2,64]{0,2,1:T(8,128)(2,1)S(1)} %get-tuple-element.16), kind=kOutput, calls=%fused_computation.116 | convolution fusion | flops 1091568640 | bytes 18890752 | tf_op jit(solution)/shard_map/sub | solution.py:82
  190.3 7.1 %fusion.29 = bf16[2,128,4,512]{3,1,2,0:T(8,128)(2,1)S(1)} fusion(bf16[1024,2,128,1]{0,2,3,1:T(8,128)(2,1)S(1)} %bitcast.112, f32[2,4,512,1024]{2,3,1,0:T(8,128)} %get-tuple-element.29, f32[2,4,512]{2,1,0:T(4,128)S(1)} %get-tuple-element.28), kind=kOutput, calls=%fused_computation.52 | convolution fusion | flops 1082654720 | bytes 18366464 | tf_op jit(solution)/shard_map/kgqs,skd->qkgd/dot_general | solution.py:84
  197.9 1.5 pad_maximum_fusion
  199.4 5.7 %all-to-all-start.1 = ((bf16[32,32,1024]{2,1,0:T(8,128)(2,1)}), bf16[32,32,1024]{2,1,0:T(8,128)(2,1)S(1)}, u32[]{:S(2)}, u32[]{:S(2)}) async-start(bf16[32,32,1024]{2,1,0:T(8,128)(2,1)} %bitcast.99), calls=%async_computation.1 | async-start | bytes 4194304 | tf_op jit(solution)/shard_map/all_to_all | solution.py:150
  205.2 30.0 %all-to-all-done.1 = bf16[32,32,1024]{2,1,0:T(8,128)(2,1)S(1)} async-done(((bf16[32,32,1024]{2,1,0:T(8,128)(2,1)}), bf16[32,32,1024]{2,1,0:T(8,128)(2,1)S(1)}, u32[]{:S(2)}, u32[]{:S(2)}) %all-to-all-start.1) | async-done | bytes 2097184 | tf_op jit(solution)/shard_map/all_to_all | solution.py:150
  235.2 2.0 gather_fusion
  237.2 8.3 %convolution_convert_fusion = bf16[512,4096]{1,0:T(8,128)(2,1)S(1)} fusion(bf16[1024,4096]{1,0:T(8,128)(2,1)} %param.13, bf16[512,1024]{1,0:T(8,128)(2,1)S(1)} %gather_fusion, pred[512]{0:T(512)(128)(4,1)S(1)} %get-tuple-element.10), kind=kOutput, calls=%fused_computation.30 | convolution fusion | flops 4297588736 | bytes 13632000 | tf_op jit(solution)/shard_map/dot_general | solution.py:158
  245.6 52.7 %all_to_all.29 = bf16[4,128,4096]{2,1,0:T(8,128)(2,1)S(1)} all-to-all(bf16[4,128,4096]{2,1,0:T(8,128)(2,1)S(1)} %bitcast.100), channel_id=1, replica_groups=mesh['dp'=32,'tp'=4] {'tp'}, dimensions={0} | all-to-all | bytes 8388608 | tf_op jit(solution)/shard_map/all_to_all | solution.py:23
  (49 shorter events, 12.0 us)
Async XLA Ops:
  0.0 168.6 %copy-start = (bf16[4096,256]{1,0:T(8,128)(2,1)S(1)}, bf16[4096,256]{1,0:T(8,128)(2,1)}, u32[]{:S(2)}) copy-start(bf16[4096,256]{1,0:T(8,128)(2,1)} %param.12) | copy-start | bytes 6291460
  23.1 12.0 %copy-start.4 = (s32[16384]{0:T(1024)S(1)}, s32[16384]{0:T(1024)}, u32[]{:S(2)}) copy-start(s32[16384]{0:T(1024)} %param.15) | copy-start | bytes 196612
  23.1 112.1 %all-to-all-start = ((bf16[128,8,4096]{2,1,0:T(8,128)(2,1)}), bf16[128,8,4096]{2,1,0:T(8,128)(2,1)}, u32[]{:S(2)}, u32[]{:S(2)}) async-start(bf16[128,8,4096]{2,1,0:T(8,128)(2,1)} %bitcast.95), calls=%async_computation | async-start | bytes 16777216 | tf_op jit(solution)/shard_map/all_to_all | solution.py:119
  148.1 1.6 copy-start.3
  168.6 8.3 %copy-start.7 = (f32[2,4,512,1024]{2,3,1,0:T(8,128)S(1)}, f32[2,4,512,1024]{2,3,1,0:T(8,128)}, u32[]{:S(2)}) copy-start(f32[2,4,512,1024]{2,3,1,0:T(8,128)} %get-tuple-element.27) | copy-start | bytes 50331652
  174.6 4.0 %copy-start.5 = (bf16[1024,256]{0,1:T(8,128)(2,1)}, bf16[1024,256]{0,1:T(8,128)(2,1)S(1)}, u32[]{:S(2)}) copy-start(bf16[1024,256]{0,1:T(8,128)(2,1)S(1)} %fusion.30) | copy-start | bytes 1572868
  179.1 11.2 %copy-start.6 = (bf16[1024,256]{0,1:T(8,128)(2,1)S(1)}, bf16[1024,256]{0,1:T(8,128)(2,1)}, u32[]{:S(2)}) copy-start(bf16[1024,256]{0,1:T(8,128)(2,1)} %copy-done.5) | copy-start | bytes 1572868
  199.4 35.8 %all-to-all-start.1 = ((bf16[32,32,1024]{2,1,0:T(8,128)(2,1)}), bf16[32,32,1024]{2,1,0:T(8,128)(2,1)S(1)}, u32[]{:S(2)}, u32[]{:S(2)}) async-start(bf16[32,32,1024]{2,1,0:T(8,128)(2,1)} %bitcast.99), calls=%async_computation.1 | async-start | bytes 4194304 | tf_op jit(solution)/shard_map/all_to_all | solution.py:150
  245.5 55.1 %copy-start.1 = (bf16[4096,256]{1,0:T(8,128)(2,1)S(1)}, bf16[4096,256]{1,0:T(8,128)(2,1)}, u32[]{:S(2)}) copy-start(bf16[4096,256]{1,0:T(8,128)(2,1)} %param.12) | copy-start | bytes 6291460
  298.2 1.2 copy-start.2
where the time goes:
time: 302 us; the launch traced here: 301 us
  waiting for transfers between devices  104 us (34%)
  matrix products  63.7 us (21%)
  blocking collectives  52.7 us (17%)
  other arithmetic  32.1 us (11%)
  local copies, waits for them, and re-layouts  29.9 us (10%)
  starting transfers between devices  17.6 us (6%)
    all_to_all x1, waiting for transfers between devices, body(): lax.all_to_all(fanned.reshape(slot_total, model_width), ('dp', 'tp'), spl...  74.4 us
    all_to_all x1, blocking collectives, sum_at_owner(): lax.all_to_all(pieces, axis, split_axis=0, concat_axis=0, tiled=True)  52.7 us
    all_to_all x1, waiting for transfers between devices, body(): lax.all_to_all(context, 'dp', split_axis=0, concat_axis=0, tiled=True)  30 us
    sub x2, matrix products, attend(): weights = jnp.exp(score_values - row_peak)  22.3 us
    dot_general x1, matrix products, body(): jnp.dot(arrived, w_query, preferred_element_type=jnp.float32)  12.9 us
    all_to_all x1, starting transfers between devices, body(): lax.all_to_all(fanned.reshape(slot_total, model_width), ('dp', 'tp'), spl...  11.9 us
    dot_general x1, local copies, waits for them, and re-layouts, body(): jnp.dot(arrived, w_query, preferred_element_type=jnp.float32)  11.5 us
    dot_general x2, matrix products, attend(): jnp.einsum('kgqs,skd->qkgd', weights, value_heads, preferred_element_type...  8.59 us
  transfers between devices with their start and end apart: 2, of which 2 were waited for; matrix products, arithmetic and copies ran while one was open for 9% of the time, Pallas kernels for 0%

commit v1 on v0

v1 whole, which is shorter than its diff:
```python
import functools
import math

import jax
import jax.numpy as jnp
from jax import lax
from jax.experimental import pallas as pl
from jax.experimental.pallas import tpu as pltpu
from jax.sharding import PartitionSpec as P

HEAD_DIM = 128
GROUP_DOCS = 4
SLOTS = 8
rope_base = 500000.0
norm_eps = 1e-05
score_floor = -1e30
MESH = pl.DeviceIdType.MESH
F32 = jnp.float32
BF16 = jnp.bfloat16


def iota(shape, dim):
    return lax.broadcasted_iota(jnp.int32, shape, dim)


def kernel(
    x_ref, gain_ref, pidx_ref, len_ref, wq_ref, wk_ref, wv_ref, wo_ref, out_ref,
    w_all, w_out, gathered, scaled, acc, sumsq, stacked, sent, arrived, qkv,
    slot_row, slot_col, slot_start, bias, unpack, mixed, back_sent, back, unpacked,
    part, half_a, half_b, from_left, from_right, own_part,
    w_sem, wo_sem, ag_send, ag_recv, send_sem, recv_sem, back_send, back_recv, rs_send, rs_recv,
):
    groups = lax.axis_size("dp")
    rows, width = x_ref.shape
    piece = width // 4
    half = width // 2
    docs = len_ref.shape[1]
    me = lax.axis_index("dp")
    z = lax.axis_index("tp")
    right = lax.rem(z + 1, 4)
    left = lax.rem(z + 3, 4)
    members = (z, left, right, lax.rem(z + 2, 4))
    q_cols = wq_ref.shape[1]
    k_cols = wk_ref.shape[1]
    heads = q_cols // HEAD_DIM
    kv_heads = k_cols // HEAD_DIM
    per_kv = heads // kv_heads
    side = (per_kv + 2) * HEAD_DIM
    ctx = per_kv * HEAD_DIM
    pack_rows = 2 * SLOTS
    nb = min(16, groups)
    chunk_slots = SLOTS * groups

    def cols(k):
        return pl.ds(k * piece, piece) if isinstance(k, int) else pl.ds(pl.multiple_of(k * piece, 128), piece)

    def w_copies(k):
        at = cols(k)
        return (
            pltpu.make_async_copy(wq_ref.at[at, :], w_all.at[at, pl.ds(0, q_cols)], w_sem.at[0, k]),
            pltpu.make_async_copy(wk_ref.at[at, :], w_all.at[at, pl.ds(q_cols, k_cols)], w_sem.at[1, k]),
            pltpu.make_async_copy(wv_ref.at[at, :], w_all.at[at, pl.ds(q_cols + k_cols, k_cols)], w_sem.at[2, k]),
        )

    for k in range(4):
        for copy in w_copies(k):
            copy.start()
    wo_copy = pltpu.make_async_copy(wo_ref, w_out, wo_sem)
    wo_copy.start()

    barrier = pltpu.get_barrier_semaphore()

    def greet(i, carry):
        pl.semaphore_signal(barrier, inc=1, device_id=(lax.rem(me + i, groups), z), device_id_type=MESH)
        return carry

    for neighbour in (right, left):
        pl.semaphore_signal(barrier, inc=1, device_id=(me, neighbour), device_id_type=MESH)
    lax.fori_loop(1, groups, greet, 0)
    pl.semaphore_wait(barrier, groups + 1)

    def column_copy(src, dst, send, recv, to):
        return pltpu.make_async_remote_copy(
            src_ref=src, dst_ref=dst, send_sem=send, recv_sem=recv, device_id=(me, to), device_id_type=MESH
        )

    def own_right(k):
        return column_copy(x_ref.at[:, cols(k)], gathered.at[0, :, cols(k)], ag_send.at[0, k], ag_recv.at[0, k], right)

    def own_left(k):
        return column_copy(x_ref.at[:, cols(k)], gathered.at[1, :, cols(k)], ag_send.at[1, k], ag_recv.at[1, k], left)

    def forward(k):
        source, to = (0, right) if k < 2 else (1, left)
        return column_copy(
            gathered.at[source, :, cols(k)], gathered.at[2, :, cols(k)], ag_send.at[2, k], ag_recv.at[2, k], to
        )

    for k in range(4):
        own_right(k).start()
        own_left((k + 2) % 4).start()

    lane = iota((1, docs), 1)
    lens_row = len_ref[...].astype(F32)
    eye_docs = iota((docs, docs), 0) == iota((docs, docs), 1)
    lens_col = jnp.sum(jnp.where(eye_docs, lens_row, 0.0), axis=1, keepdims=True)
    before = iota((docs, docs), 0) < iota((docs, docs), 1)
    starts_row = jnp.sum(jnp.where(before, lens_col, 0.0), axis=0, keepdims=True)
    group_of = iota((groups, docs), 0)
    lane_g = iota((groups, docs), 1)
    group_lo = jnp.sum(jnp.where(lane_g < GROUP_DOCS * group_of, lens_row, 0.0), axis=1, keepdims=True)
    group_hi = jnp.sum(jnp.where(lane_g < GROUP_DOCS * (group_of + 1), lens_row, 0.0), axis=1, keepdims=True)

    def upto(count):
        return jnp.sum(jnp.where(lane < count, lens_row, 0.0), axis=1, keepdims=True)

    my_lo = upto(GROUP_DOCS * me)
    my_hi = upto(GROUP_DOCS * (me + 1))
    my_starts = [upto(GROUP_DOCS * me + i) - my_lo for i in range(1, GROUP_DOCS)]
    earlier = (iota((rows, rows), 0) < iota((rows, rows), 1)).astype(BF16)
    spread_p = (iota((pack_rows * groups, groups), 0) // pack_rows == iota((pack_rows * groups, groups), 1)).astype(BF16)
    spread_s = (iota((chunk_slots, groups), 0) // SLOTS == iota((chunk_slots, groups), 1)).astype(BF16)

    def dot(a, b):
        return jnp.dot(a, b, preferred_element_type=F32)

    def slot_tables(c):
        index = pidx_ref[members[c], :, :].astype(F32)
        mine = (index >= my_lo) & (index < my_hi)
        rank = dot(jnp.where(mine, 1.0, 0.0).astype(BF16), earlier)
        code = jnp.where(mine, rank, -1.0).astype(BF16)
        place = jnp.where(mine, index - my_lo, 0.0)
        high = jnp.floor(place * (1.0 / 32.0))
        low = place - high * 32.0
        code_s = dot(spread_s, code)
        place_s = dot(spread_s, high.astype(BF16)) * 32.0 + dot(spread_s, low.astype(BF16))
        wanted = (iota((chunk_slots, rows), 0) % SLOTS).astype(F32)
        found = jnp.sum(jnp.where(code_s == wanted, place_s + 1.0, 0.0), axis=1, keepdims=True) - 1.0
        begin = jnp.zeros_like(found)
        for start in my_starts:
            begin = jnp.where(found >= start, start, begin)
        slot_col[c] = jnp.broadcast_to(found, (chunk_slots, 128))
        slot_start[c] = jnp.broadcast_to(begin, (chunk_slots, 128))
        same = iota((chunk_slots, chunk_slots), 0) == iota((chunk_slots, chunk_slots), 1)
        slot_row[:, pl.ds(c * chunk_slots, chunk_slots)] = jnp.sum(jnp.where(same, found, 0.0), axis=0, keepdims=True)

    sumsq[...] = jnp.zeros_like(sumsq)
    acc[...] = jnp.zeros_like(acc)
    total_cols = q_cols + 2 * k_cols
    n_tile = 512

    def project(c, k):
        at = cols(k)
        x = (x_ref[:, at] if c == 0 else gathered[c - 1, :, at]).astype(F32)
        squares = sumsq[c]
        for j in range(piece // 128):
            block = x[:, j * 128 : (j + 1) * 128]
            squares = squares + block * block
        sumsq[c] = squares
        scaled[...] = (x * gain_ref[:, at]).astype(BF16)
        for n in range(total_cols // n_tile):
            to = pl.ds(n * n_tile, n_tile)
            acc[c, :, to] += dot(scaled[...], w_all[at, to])

    def dispatch(c):
        scale = lax.rsqrt(jnp.sum(sumsq[c], axis=1, keepdims=True) * (1.0 / width) + norm_eps)
        index = pidx_ref[members[c], pl.ds(me, 1), :].astype(F32)
        eye = iota((rows, rows), 0) == iota((rows, rows), 1)
        index_col = jnp.sum(jnp.where(eye, index, 0.0), axis=1, keepdims=True)
        begin = jnp.max(jnp.where(starts_row <= index_col, starts_row, 0.0), axis=1, keepdims=True)
        place = index_col - begin
        lanes = iota((1, HEAD_DIM), 1)
        exponent = (lanes % (HEAD_DIM // 2)).astype(F32) * (-2.0 * math.log(rope_base) / HEAD_DIM)
        angle = place * jnp.exp(exponent)
        cosine = jnp.cos(angle)
        sine = jnp.where(lanes < HEAD_DIM // 2, -1.0, 1.0) * jnp.sin(angle)

        def head(column):
            return acc[c, :, pl.ds(column * HEAD_DIM, HEAD_DIM)] * scale

        def rope(t):
            return t * cosine + pltpu.roll(t, HEAD_DIM // 2, 1) * sine

        for g in range(kv_heads):
            at = pl.ds(g * rows, rows)
            for j in range(per_kv):
                stacked[at, pl.ds(j * HEAD_DIM, HEAD_DIM)] = rope(head(g * per_kv + j)).astype(BF16)
            stacked[at, pl.ds(ctx, HEAD_DIM)] = rope(head(heads + g)).astype(BF16)
            stacked[at, pl.ds(ctx + HEAD_DIM, HEAD_DIM)] = head(heads + kv_heads + g).astype(BF16)

        inside = (index >= group_lo) & (index < group_hi)
        rank = dot(jnp.where(inside, 1.0, 0.0).astype(BF16), earlier)
        code = jnp.where(inside, rank, -100.0).astype(BF16)
        spread = dot(spread_p, code)
        wanted = (iota((pack_rows * groups, rows), 0) % pack_rows).astype(F32)
        pick = [jnp.where(spread + float(SLOTS * g) == wanted, 1.0, 0.0) for g in range(2)]
        for g in range(2):
            unpack[c, pl.ds(g * rows, rows), :] = jnp.transpose(pick[g]).astype(BF16)
        pick = jnp.concatenate(pick, axis=1).astype(BF16)
        for b in range(groups // nb):
            block = pick[b * nb * pack_rows : (b + 1) * nb * pack_rows]
            sent[pl.ds(c * groups + b * nb, nb)] = (
                dot(block, stacked[...]).astype(BF16).reshape(nb, pack_rows, side)
            )
        arrived[c * groups + me] = sent[c * groups + me]

        def send(i, carry):
            to = lax.rem(me + i, groups)
            pltpu.make_async_remote_copy(
                src_ref=sent.at[c * groups + to],
                dst_ref=arrived.at[c * groups + me],
                send_sem=send_sem.at[c],
                recv_sem=recv_sem.at[c],
                device_id=(to, z),
                device_id_type=MESH,
            ).start()
            return carry

        lax.fori_loop(1, groups, send, 0)

    def all_but_one(ref, c, sem):
        block = ref.at[pl.ds(c * groups, groups - 1)]
        pltpu.make_async_copy(block, block, sem.at[c]).wait()

    reorder_rows = pack_rows * nb
    out_row = iota((reorder_rows, reorder_rows), 0)
    in_row = iota((reorder_rows, reorder_rows), 1)
    split = nb * SLOTS
    source_row = (out_row % split) // SLOTS * pack_rows + out_row // split * SLOTS + out_row % SLOTS
    apart = (source_row == in_row).astype(BF16)
    source_back = (in_row % split) // SLOTS * pack_rows + in_row // split * SLOTS + in_row % SLOTS
    together = (source_back == out_row).astype(BF16)

    def receive(c):
        all_but_one(arrived, c, recv_sem)
        for b in range(groups // nb):
            block = arrived[pl.ds(c * groups + b * nb, nb)].reshape(reorder_rows, side)
            ordered = dot(apart, block).astype(BF16)
            for g in range(2):
                qkv[g, pl.ds(c * chunk_slots + b * split, split), :] = ordered[g * split : (g + 1) * split]

    def attend(c):
        found = slot_col[c][:, :1]
        begin = slot_start[c][:, :1]
        keys = slot_row[...]
        bias[...] = jnp.where((keys >= begin) & (keys <= found), 0.0, score_floor)
        at = pl.ds(c * chunk_slots, chunk_slots)

        def one_head(i, carry):
            g = i // per_kv
            lanes = pl.ds(pl.multiple_of(i % per_kv * HEAD_DIM, HEAD_DIM), HEAD_DIM)
            query = qkv[g, at, lanes]
            key = qkv[g, :, pl.ds(ctx, HEAD_DIM)]
            value = qkv[g, :, pl.ds(ctx + HEAD_DIM, HEAD_DIM)]
            scores = lax.dot_general(query, key, (((1,), (1,)), ((), ())), preferred_element_type=F32)
            scores = scores * HEAD_DIM ** (-0.5) + bias[...]
            weights = jnp.exp(scores - jnp.max(scores, axis=1, keepdims=True))
            total = jnp.sum(weights, axis=1, keepdims=True)
            mixed[g, :, lanes] = (dot(weights.astype(BF16), value) / total).astype(BF16)
            return carry

        lax.fori_loop(0, heads, one_head, 0)
        for b in range(groups // nb):
            block = mixed[:, pl.ds(b * split, split), :].reshape(reorder_rows, ctx)
            back_sent[pl.ds(c * groups + b * nb, nb)] = dot(together, block).astype(BF16).reshape(nb, pack_rows, ctx)
        back[c * groups + me] = back_sent[c * groups + me]

        def send(i, carry):
            to = lax.rem(me + i, groups)
            pltpu.make_async_remote_copy(
                src_ref=back_sent.at[c * groups + to],
                dst_ref=back.at[c * groups + me],
                send_sem=back_send.at[c],
                recv_sem=back_recv.at[c],
                device_id=(to, z),
                device_id_type=MESH,
            ).start()
            return carry

        lax.fori_loop(1, groups, send, 0)

    o_tile = min(512, half)
    per_half = half // o_tile

    def fetch(c):
        all_but_one(back, c, back_recv)
        block = back[pl.ds(c * groups, groups)].reshape(pack_rows * groups, ctx)
        both = dot(unpack[c], block).astype(BF16)
        for g in range(2):
            unpacked[:, pl.ds(g * ctx, ctx)] = both[g * rows : (g + 1) * rows]

    def tile(n):
        return pl.ds(pl.multiple_of(n * o_tile, 128), o_tile)

    def output_half(c, which, extra):
        def step(n, carry):
            at = tile(which * per_half + n)
            value = dot(unpacked[...], w_out[:, at])
            if extra is not None:
                value = value + extra[:, tile(n)].astype(F32)
            part[c - 1, :, at] = value.astype(BF16)
            return carry

        lax.fori_loop(0, per_half, step, 0)

    halves = (pl.ds(0, half), pl.ds(half, half))
    sums = {
        "a": lambda: column_copy(part.at[2, :, halves[0]], half_a, rs_send.at[0], rs_recv.at[0], right),
        "b": lambda: column_copy(part.at[2, :, halves[1]], half_b, rs_send.at[1], rs_recv.at[1], left),
        "r0": lambda: column_copy(part.at[1, :, halves[0]], from_left.at[:, halves[0]], rs_send.at[2], rs_recv.at[2], right),
        "r1": lambda: column_copy(part.at[1, :, halves[1]], from_left.at[:, halves[1]], rs_send.at[3], rs_recv.at[3], right),
        "l0": lambda: column_copy(part.at[0, :, halves[0]], from_right.at[:, halves[0]], rs_send.at[4], rs_recv.at[4], left),
        "l1": lambda: column_copy(part.at[0, :, halves[1]], from_right.at[:, halves[1]], rs_send.at[5], rs_recv.at[5], left),
    }

    with jax.named_scope("own_chunk"):
        for k in range(4):
            for copy in w_copies(k):
                copy.wait()
            project(0, k)
        dispatch(0)
    with jax.named_scope("tables"):
        for c in range(4):
            slot_tables(c)
    with jax.named_scope("neighbour_chunks"):
        for j in range(4):
            k, m = j, (j + 2) % 4
            own_right(k).wait_recv()
            if k < 2:
                forward(k).start()
            own_left(m).wait_recv()
            if m >= 2:
                forward(m).start()
            project(1, k)
            project(2, m)
        dispatch(1)
        dispatch(2)
    receive(0)
    with jax.named_scope("far_chunk"):
        for k in (0, 2, 1, 3):
            forward(k).wait_recv()
            project(3, k)
        dispatch(3)
    for c in range(1, 4):
        receive(c)
    wo_copy.wait()
    with jax.named_scope("attend"):
        attend(3)
        attend(2)
        fetch(3)
        output_half(3, 0, None)
        sums["a"]().start()
        output_half(3, 1, None)
        sums["b"]().start()
        attend(1)
        fetch(2)
        output_half(2, 1, None)
        sums["r1"]().start()
        sums["a"]().wait_recv()
        output_half(2, 0, half_a)
        sums["r0"]().start()
        attend(0)
        fetch(1)
        output_half(1, 0, None)
        sums["l0"]().start()
        sums["b"]().wait_recv()
        output_half(1, 1, half_b)
        sums["l1"]().start()
        fetch(0)

    def own_step(n, carry):
        at = tile(n)
        own_part[:, at] = x_ref[:, at].astype(F32) + dot(unpacked[...], w_out[:, at])
        return carry

    lax.fori_loop(0, 2 * per_half, own_step, 0)

    def finish(which):
        def step(n, carry):
            at = tile(which * per_half + n)
            out_ref[:, at] = (
                own_part[:, at] + from_left[:, at].astype(F32) + from_right[:, at].astype(F32)
            ).astype(BF16)
            return carry

        lax.fori_loop(0, per_half, step, 0)

    for which in range(2):
        sums[f"r{which}"]().wait_recv()
        sums[f"l{which}"]().wait_recv()
        finish(which)

    for k in range(4):
        own_right(k).wait_send()
        own_left(k).wait_send()
        forward(k).wait_send()
    for c in range(4):
        all_but_one(sent, c, send_sem)
        all_but_one(back_sent, c, back_send)
    for copy in sums.values():
        copy().wait_send()


def body(tokens, norm_gain, w_query, w_key, w_value, w_output, doc_lengths, pack_index):
    groups = lax.axis_size("dp")
    members = lax.axis_size("tp")
    rows, width = tokens.shape
    piece = width // 4
    q_cols, k_cols = w_query.shape[1], w_key.shape[1]
    total_cols = q_cols + 2 * k_cols
    per_kv = q_cols // k_cols
    side = (per_kv + 2) * HEAD_DIM
    ctx = per_kv * HEAD_DIM
    chunk_slots = SLOTS * groups
    index = jnp.swapaxes(pack_index.reshape(groups, members, rows), 0, 1)
    vmem = pl.BlockSpec(memory_space=pltpu.VMEM)
    hbm = pl.BlockSpec(memory_space=pl.ANY)
    dma = pltpu.SemaphoreType.DMA
    V = pltpu.VMEM
    return pl.pallas_call(
        kernel,
        out_shape=jax.ShapeDtypeStruct((rows, width), BF16),
        in_specs=[vmem, vmem, vmem, vmem, hbm, hbm, hbm, hbm],
        out_specs=vmem,
        scratch_shapes=[
            V((width, total_cols), BF16),
            V(w_output.shape, BF16),
            V((3, rows, width), BF16),
            V((rows, piece), BF16),
            V((4, rows, total_cols), F32),
            V((4, rows, 128), F32),
            V((2 * rows, side), BF16),
            V((4 * groups, 2 * SLOTS, side), BF16),
            V((4 * groups, 2 * SLOTS, side), BF16),
            V((2, 4 * chunk_slots, side), BF16),
            V((1, 4 * chunk_slots), F32),
            V((4, chunk_slots, 128), F32),
            V((4, chunk_slots, 128), F32),
            V((chunk_slots, 4 * chunk_slots), F32),
            V((4, 2 * rows, 2 * SLOTS * groups), BF16),
            V((2, chunk_slots, ctx), BF16),
            V((4 * groups, 2 * SLOTS, ctx), BF16),
            V((4 * groups, 2 * SLOTS, ctx), BF16),
            V((rows, 2 * ctx), BF16),
            V((3, rows, width), BF16),
            V((rows, width // 2), BF16),
            V((rows, width // 2), BF16),
            V((rows, width), BF16),
            V((rows, width), BF16),
            V((rows, width), F32),
            dma((3, 4)),
            dma,
            dma((3, 4)),
            dma((3, 4)),
            dma((4,)),
            dma((4,)),
            dma((4,)),
            dma((4,)),
            dma((6,)),
            dma((6,)),
        ],
        compiler_params=pltpu.CompilerParams(
            collective_id=0, has_side_effects=True, vmem_limit_bytes=67043328
        ),
        name="packed_attention",
    )(tokens, norm_gain.reshape(1, width), index, doc_lengths.reshape(1, -1), w_query, w_key, w_value, w_output)


def solution(mesh):
    placed = (
        P(("dp", "tp"), None),
        P(),
        P(None, "tp"),
        P(None, "tp"),
        P(None, "tp"),
        P("tp", None),
        P(),
        P(),
    )
    return jax.shard_map(
        body, mesh=mesh, in_specs=placed, out_specs=P(("dp", "tp"), None), check_vma=False
    )
```

time: 302 us -> 132 us (0.44)
  Pallas kernels: 0 us -> 128 us
  waiting for transfers between devices: 104 us -> 0 us
  matrix products: 63.7 us -> 0 us
  blocking collectives: 52.7 us -> 0 us
  other arithmetic: 32.1 us -> 0 us
  local copies, waits for them, and re-layouts: 29.9 us -> 3.76 us
  starting transfers between devices: 17.6 us -> 0 us
    pallas_call x0 -> x1, Pallas kernels: none -> 128 us  [body(): pl.pallas_call(kernel, out_shape=jax.ShapeDtypeStruct((rows, width), BF16...]
    all_to_all x2 -> x0, waiting for transfers between devices: 104 us -> none  [the longest x1 74.4 us: body(): lax.all_to_all(fanned.reshape(slot_total, model_width), ('dp', 'tp'), spl...]
    all_to_all x1 -> x0, blocking collectives: 52.7 us -> none  [sum_at_owner(): lax.all_to_all(pieces, axis, split_axis=0, concat_axis=0, tiled=True)]
    dot_general x6 -> x0, matrix products: 41.4 us -> none  [the longest x1 12.9 us: body(): jnp.dot(arrived, w_query, preferred_element_type=jnp.float32)]
    sub x2 -> x0, matrix products: 22.3 us -> none  [attend(): weights = jnp.exp(score_values - row_peak)]
    all_to_all x2 -> x0, starting transfers between devices: 17.6 us -> none  [the longest x1 11.9 us: body(): lax.all_to_all(fanned.reshape(slot_total, model_width), ('dp', 'tp'), spl...]
    reduce_sum x4 -> x0, other arithmetic: 16.9 us -> none  [the longest x1 8.03 us: row_tables(): position = pack_index - jnp.sum(inside * doc_starts[None, :], axis=1)]
    dot_general x2 -> x0, local copies, waits for them, and re-layouts: 15.6 us -> none  [the longest x1 11.5 us: body(): jnp.dot(arrived, w_query, preferred_element_type=jnp.float32)]
  transfers between devices with their start and end apart: 2 -> 0, of which waited for: 2 -> 0; matrix products, arithmetic and copies ran while one was open for 9% -> 0% of each run, Pallas kernels for 0% -> 0%
where the time goes in v1:
time: 132 us
  Pallas kernels  128 us (97%)
  local copies, waits for them, and re-layouts  3.76 us (3%)
    pallas_call x1, Pallas kernels, body(): pl.pallas_call(kernel, out_shape=jax.ShapeDtypeStruct((rows, width), BF16...  128 us

profile of v1, /device:TPU:0, one launch (start us, length us, event | category | flops | bytes accessed | tf_op | source)
XLA Modules:
  0.0 132.2 jit_solution(8971456453871439103)
XLA Ops:
  0.0 1.5 %copy.11 = s32[32,4,128]{2,0,1:T(8,128)} copy(s32[32,4,128]{2,1,0:T(4,128)} %bitcast.7) | data formatting | bytes 131072 | tf_op jit(solution)/shard_map/reshape | solution.py:415
  1.5 128.4 %packed_attention.1 = bf16[128,4096]{1,0:T(8,128)(2,1)} custom-call(bf16[128,4096]{1,0:T(8,128)(2,1)} %x_ref.1, f32[1,4096]{1,0:T(1,128)} %bitcast.8, s32[4,32,128]{2,1,0:T(8,128)} %bitcast.6, s32[1,128]{1,0:T(1,128)} %bitcast.9, bf16[4096,1024]{1,0:T(8,128)(2,1)} %wq_ref.1, bf16[4096,256]{1,0:T(8,128)(2,1)} %wk_ref.1, bf16[4096,256]{1,0:T(8,128)(2,1)} %wv_ref.1, ...), custom_call_target="tpu_custom_call" | custom-call | tf_op jit(solution)/shard_map/packed_attention/pallas_call | solution.py:420
  129.9 2.3 %copy.13 = bf16[128,4096]{1,0:T(8,128)(2,1)} copy(bf16[128,4096]{1,0:T(8,128)(2,1)} %packed_attention.1) | data formatting | bytes 2097152

commit v2 on v1

--- a/solution.py
+++ b/solution.py
@@ -24,11 +24,13 @@
 
 
 def kernel(
-    x_ref, gain_ref, pidx_ref, len_ref, wq_ref, wk_ref, wv_ref, wo_ref, out_ref,
-    w_all, w_out, gathered, scaled, acc, sumsq, stacked, sent, arrived, qkv,
+    x_hbm, gain_hbm, pidx_hbm, len_hbm, wq_ref, wk_ref, wv_ref, wo_ref, out_hbm,
+    x_ref, gain_ref, pidx_ref, len_ref, partner_x, out_ref,
+    w_all, w_out, gathered, scaled, acc, sumsq, stacked, cosines, sines, picks, sent, arrived, qkv,
     slot_row, slot_col, slot_start, bias, unpack, mixed, back_sent, back, unpacked,
     part, half_a, half_b, from_left, from_right, own_part,
-    w_sem, wo_sem, ag_send, ag_recv, send_sem, recv_sem, back_send, back_recv, rs_send, rs_recv,
+    in_sem, out_sem, w_sem, wo_sem, pair_send, pair_recv, ag_send, ag_recv,
+    send_sem, recv_sem, back_send, back_recv, rs_send, rs_recv,
 ):
     groups = lax.axis_size("dp")
     rows, width = x_ref.shape
@@ -39,7 +41,15 @@
     z = lax.axis_index("tp")
     right = lax.rem(z + 1, 4)
     left = lax.rem(z + 3, 4)
-    members = (z, left, right, lax.rem(z + 2, 4))
+    core = lax.rem(me, 2)
+    partner = me + 1 - 2 * core
+    ahead = lax.rem(z + 1 + 2 * core, 4)
+    behind = lax.rem(z + 3 - 2 * core, 4)
+    first, second = core, 1 - core
+
+    def member(c):
+        return lax.rem(z + c // 3 * 2 + (c % 3 + 1) // 2 * (1 + 2 * (c % 2)), 4)
+
     q_cols = wq_ref.shape[1]
     k_cols = wk_ref.shape[1]
     heads = q_cols // HEAD_DIM
@@ -62,6 +72,14 @@
             pltpu.make_async_copy(wv_ref.at[at, :], w_all.at[at, pl.ds(q_cols + k_cols, k_cols)], w_sem.at[2, k]),
         )
 
+    loads = [
+        pltpu.make_async_copy(src, dst, in_sem.at[i])
+        for i, (src, dst) in enumerate(
+            ((x_hbm, x_ref), (gain_hbm, gain_ref), (pidx_hbm, pidx_ref), (len_hbm, len_ref))
+        )
+    ]
+    for copy in loads:
+        copy.start()
     for k in range(4):
         for copy in w_copies(k):
             copy.start()
@@ -74,31 +92,46 @@
         pl.semaphore_signal(barrier, inc=1, device_id=(lax.rem(me + i, groups), z), device_id_type=MESH)
         return carry
 
-    for neighbour in (right, left):
-        pl.semaphore_signal(barrier, inc=1, device_id=(me, neighbour), device_id_type=MESH)
+    for device in ((me, right), (me, left), (partner, ahead)):
+        pl.semaphore_signal(barrier, inc=1, device_id=device, device_id_type=MESH)
     lax.fori_loop(1, groups, greet, 0)
-    pl.semaphore_wait(barrier, groups + 1)
+    for copy in loads:
+        copy.wait()
+    pl.semaphore_wait(barrier, groups + 2)
+
+    def copy_to(src, dst, send, recv, device):
+        return pltpu.make_async_remote_copy(
+            src_ref=src, dst_ref=dst, send_sem=send, recv_sem=recv, device_id=device, device_id_type=MESH
+        )
 
     def column_copy(src, dst, send, recv, to):
-        return pltpu.make_async_remote_copy(
-            src_ref=src, dst_ref=dst, send_sem=send, recv_sem=recv, device_id=(me, to), device_id_type=MESH
+        return copy_to(src, dst, send, recv, (me, to))
+
+    def own_ahead(k):
+        return copy_to(
+            x_ref.at[:, cols(k)], gathered.at[first, :, cols(k)], ag_send.at[0, k], ag_recv.at[first, k], (me, ahead)
         )
 
-    def own_right(k):
-        return column_copy(x_ref.at[:, cols(k)], gathered.at[0, :, cols(k)], ag_send.at[0, k], ag_recv.at[0, k], right)
-
-    def own_left(k):
-        return column_copy(x_ref.at[:, cols(k)], gathered.at[1, :, cols(k)], ag_send.at[1, k], ag_recv.at[1, k], left)
-
-    def forward(k):
-        source, to = (0, right) if k < 2 else (1, left)
-        return column_copy(
-            gathered.at[source, :, cols(k)], gathered.at[2, :, cols(k)], ag_send.at[2, k], ag_recv.at[2, k], to
+    def to_partner(k):
+        return copy_to(x_ref.at[:, cols(k)], partner_x.at[:, cols(k)], pair_send.at[k], pair_recv.at[k], (partner, z))
+
+    def partner_ahead(k):
+        return copy_to(
+            partner_x.at[:, cols(k)], gathered.at[first, :, cols(k)], ag_send.at[1, k], ag_recv.at[first, k], (partner, ahead)
         )
 
+    def landed(slot, k):
+        piece_ref = gathered.at[slot, :, cols(k)]
+        pltpu.make_async_copy(piece_ref, piece_ref, ag_recv.at[slot, k]).wait()
+
+    def forward(slot, j, to):
+        k = 2 * slot + j
+        source = gathered.at[slot, :, cols(k)]
+        return copy_to(source, gathered.at[2, :, cols(k)], ag_send.at[2, k], ag_recv.at[2, k], (me, to))
+
     for k in range(4):
-        own_right(k).start()
-        own_left((k + 2) % 4).start()
+        own_ahead(k).start()
+        to_partner(k).start()
 
     lane = iota((1, docs), 1)
     lens_row = len_ref[...].astype(F32)
@@ -125,7 +158,7 @@
         return jnp.dot(a, b, preferred_element_type=F32)
 
     def slot_tables(c):
-        index = pidx_ref[members[c], :, :].astype(F32)
+        index = pidx_ref[pl.ds(member(c), groups, stride=4), :].astype(F32)
         mine = (index >= my_lo) & (index < my_hi)
         rank = dot(jnp.where(mine, 1.0, 0.0).astype(BF16), earlier)
         code = jnp.where(mine, rank, -1.0).astype(BF16)
@@ -149,9 +182,9 @@
     total_cols = q_cols + 2 * k_cols
     n_tile = 512
 
-    def project(c, k):
+    def project(c, k, x):
         at = cols(k)
-        x = (x_ref[:, at] if c == 0 else gathered[c - 1, :, at]).astype(F32)
+        x = x.astype(F32)
         squares = sumsq[c]
         for j in range(piece // 128):
             block = x[:, j * 128 : (j + 1) * 128]
@@ -162,9 +195,8 @@
             to = pl.ds(n * n_tile, n_tile)
             acc[c, :, to] += dot(scaled[...], w_all[at, to])
 
-    def dispatch(c):
-        scale = lax.rsqrt(jnp.sum(sumsq[c], axis=1, keepdims=True) * (1.0 / width) + norm_eps)
-        index = pidx_ref[members[c], pl.ds(me, 1), :].astype(F32)
+    def prepare(c):
+        index = pidx_ref[pl.ds(4 * me + member(c), 1), :].astype(F32)
         eye = iota((rows, rows), 0) == iota((rows, rows), 1)
         index_col = jnp.sum(jnp.where(eye, index, 0.0), axis=1, keepdims=True)
         begin = jnp.max(jnp.where(starts_row <= index_col, starts_row, 0.0), axis=1, keepdims=True)
@@ -172,33 +204,38 @@
         lanes = iota((1, HEAD_DIM), 1)
         exponent = (lanes % (HEAD_DIM // 2)).astype(F32) * (-2.0 * math.log(rope_base) / HEAD_DIM)
         angle = place * jnp.exp(exponent)
-        cosine = jnp.cos(angle)
-        sine = jnp.where(lanes < HEAD_DIM // 2, -1.0, 1.0) * jnp.sin(angle)
-
-        def head(column):
-            return acc[c, :, pl.ds(column * HEAD_DIM, HEAD_DIM)] * scale
-
-        def rope(t):
-            return t * cosine + pltpu.roll(t, HEAD_DIM // 2, 1) * sine
-
-        for g in range(kv_heads):
-            at = pl.ds(g * rows, rows)
-            for j in range(per_kv):
-                stacked[at, pl.ds(j * HEAD_DIM, HEAD_DIM)] = rope(head(g * per_kv + j)).astype(BF16)
-            stacked[at, pl.ds(ctx, HEAD_DIM)] = rope(head(heads + g)).astype(BF16)
-            stacked[at, pl.ds(ctx + HEAD_DIM, HEAD_DIM)] = head(heads + kv_heads + g).astype(BF16)
-
+        cosines[c] = jnp.cos(angle)
+        sines[c] = jnp.where(lanes < HEAD_DIM // 2, -1.0, 1.0) * jnp.sin(angle)
         inside = (index >= group_lo) & (index < group_hi)
         rank = dot(jnp.where(inside, 1.0, 0.0).astype(BF16), earlier)
         code = jnp.where(inside, rank, -100.0).astype(BF16)
         spread = dot(spread_p, code)
         wanted = (iota((pack_rows * groups, rows), 0) % pack_rows).astype(F32)
-        pick = [jnp.where(spread + float(SLOTS * g) == wanted, 1.0, 0.0) for g in range(2)]
         for g in range(2):
-            unpack[c, pl.ds(g * rows, rows), :] = jnp.transpose(pick[g]).astype(BF16)
-        pick = jnp.concatenate(pick, axis=1).astype(BF16)
+            pick = jnp.where(spread + float(SLOTS * g) == wanted, 1.0, 0.0)
+            unpack[c, pl.ds(g * rows, rows), :] = jnp.transpose(pick).astype(BF16)
+            picks[c, :, pl.ds(g * rows, rows)] = pick.astype(BF16)
+
+    def dispatch(c):
+        scale = lax.rsqrt(jnp.sum(sumsq[c], axis=1, keepdims=True) * (1.0 / width) + norm_eps)
+        cosine = cosines[c]
+        sine = sines[c]
+        query_scale = scale * (HEAD_DIM ** (-0.5) / math.log(2.0))
+
+        def head(column, by):
+            return acc[c, :, pl.ds(column * HEAD_DIM, HEAD_DIM)] * by
+
+        def rope(t):
+            return t * cosine + pltpu.roll(t, HEAD_DIM // 2, 1) * sine
+
+        for g in range(kv_heads):
+            at = pl.ds(g * rows, rows)
+            for j in range(per_kv):
+                stacked[at, pl.ds(j * HEAD_DIM, HEAD_DIM)] = rope(head(g * per_kv + j, query_scale)).astype(BF16)
+            stacked[at, pl.ds(ctx, HEAD_DIM)] = rope(head(heads + g, scale)).astype(BF16)
+            stacked[at, pl.ds(ctx + HEAD_DIM, HEAD_DIM)] = head(heads + kv_heads + g, scale).astype(BF16)
         for b in range(groups // nb):
-            block = pick[b * nb * pack_rows : (b + 1) * nb * pack_rows]
+            block = picks[c, pl.ds(b * nb * pack_rows, nb * pack_rows), :]
             sent[pl.ds(c * groups + b * nb, nb)] = (
                 dot(block, stacked[...]).astype(BF16).reshape(nb, pack_rows, side)
             )
@@ -237,29 +274,28 @@
             block = arrived[pl.ds(c * groups + b * nb, nb)].reshape(reorder_rows, side)
             ordered = dot(apart, block).astype(BF16)
             for g in range(2):
-                qkv[g, pl.ds(c * chunk_slots + b * split, split), :] = ordered[g * split : (g + 1) * split]
-
-    def attend(c):
+                qkv[g, pl.ds(c * chunk_slots + b * split, split), pl.ds(0, side)] = ordered[g * split : (g + 1) * split]
+
+    def mask(c):
         found = slot_col[c][:, :1]
         begin = slot_start[c][:, :1]
         keys = slot_row[...]
         bias[...] = jnp.where((keys >= begin) & (keys <= found), 0.0, score_floor)
+
+    def attend(c):
         at = pl.ds(c * chunk_slots, chunk_slots)
 
-        def one_head(i, carry):
+        for i in range(heads):
             g = i // per_kv
-            lanes = pl.ds(pl.multiple_of(i % per_kv * HEAD_DIM, HEAD_DIM), HEAD_DIM)
+            lanes = pl.ds(i % per_kv * HEAD_DIM, HEAD_DIM)
             query = qkv[g, at, lanes]
             key = qkv[g, :, pl.ds(ctx, HEAD_DIM)]
-            value = qkv[g, :, pl.ds(ctx + HEAD_DIM, HEAD_DIM)]
+            value = qkv[g, :, pl.ds(ctx + HEAD_DIM, 2 * HEAD_DIM)]
             scores = lax.dot_general(query, key, (((1,), (1,)), ((), ())), preferred_element_type=F32)
-            scores = scores * HEAD_DIM ** (-0.5) + bias[...]
-            weights = jnp.exp(scores - jnp.max(scores, axis=1, keepdims=True))
-            total = jnp.sum(weights, axis=1, keepdims=True)
-            mixed[g, :, lanes] = (dot(weights.astype(BF16), value) / total).astype(BF16)
-            return carry
-
-        lax.fori_loop(0, heads, one_head, 0)
+            scores = scores + bias[...]
+            weights = jnp.exp2(scores - jnp.max(scores, axis=1, keepdims=True))
+            both = dot(weights.astype(BF16), value)
+            mixed[g, :, lanes] = (both[:, :HEAD_DIM] / both[:, HEAD_DIM:]).astype(BF16)
         for b in range(groups // nb):
             block = mixed[:, pl.ds(b * split, split), :].reshape(reorder_rows, ctx)
             back_sent[pl.ds(c * groups + b * nb, nb)] = dot(together, block).astype(BF16).reshape(nb, pack_rows, ctx)
@@ -287,7 +323,7 @@
         block = back[pl.ds(c * groups, groups)].reshape(pack_rows * groups, ctx)
         both = dot(unpack[c], block).astype(BF16)
         for g in range(2):
-            unpacked[:, pl.ds(g * ctx, ctx)] = both[g * rows : (g + 1) * rows]
+            unpacked[c, :, pl.ds(g * ctx, ctx)] = both[g * rows : (g + 1) * rows]
 
     def tile(n):
         return pl.ds(pl.multiple_of(n * o_tile, 128), o_tile)
@@ -295,7 +331,7 @@
     def output_half(c, which, extra):
         def step(n, carry):
             at = tile(which * per_half + n)
-            value = dot(unpacked[...], w_out[:, at])
+            value = dot(unpacked[c], w_out[:, at])
             if extra is not None:
                 value = value + extra[:, tile(n)].astype(F32)
             part[c - 1, :, at] = value.astype(BF16)
@@ -313,64 +349,85 @@
         "l1": lambda: column_copy(part.at[0, :, halves[1]], from_right.at[:, halves[1]], rs_send.at[5], rs_recv.at[5], left),
     }
 
-    with jax.named_scope("own_chunk"):
-        for k in range(4):
-            for copy in w_copies(k):
-                copy.wait()
-            project(0, k)
-        dispatch(0)
-    with jax.named_scope("tables"):
-        for c in range(4):
-            slot_tables(c)
-    with jax.named_scope("neighbour_chunks"):
-        for j in range(4):
-            k, m = j, (j + 2) % 4
-            own_right(k).wait_recv()
-            if k < 2:
-                forward(k).start()
-            own_left(m).wait_recv()
-            if m >= 2:
-                forward(m).start()
-            project(1, k)
-            project(2, m)
-        dispatch(1)
-        dispatch(2)
+    for k in range(4):
+        for copy in w_copies(k):
+            copy.wait()
+        project(0, k, x_ref[:, cols(k)])
+    prepare(0)
+    dispatch(0)
+    for k in range(4):
+        to_partner(k).wait_recv()
+        partner_ahead(k).start()
+    for c in range(1, 4):
+        prepare(c)
+    for c in range(4):
+        slot_tables(c)
+    for g in range(2):
+        qkv[g, :, pl.ds(side, HEAD_DIM)] = jnp.ones((4 * chunk_slots, HEAD_DIM), BF16)
+    mask(3)
+
+    def first_piece(k, carry):
+        landed(first, k)
+        project(1 + first, k, gathered[first, :, cols(k)])
+        return carry
+
+    lax.fori_loop(0, 4, first_piece, 0)
+    for j in range(2):
+        forward(first, j, ahead).start()
+    dispatch(1 + first)
     receive(0)
-    with jax.named_scope("far_chunk"):
-        for k in (0, 2, 1, 3):
-            forward(k).wait_recv()
-            project(3, k)
-        dispatch(3)
-    for c in range(1, 4):
-        receive(c)
+
+    def second_piece(k, carry):
+        landed(second, k)
+        project(1 + second, k, gathered[second, :, cols(k)])
+        return carry
+
+    lax.fori_loop(0, 4, second_piece, 0)
+    for j in range(2):
+        forward(second, j, behind).start()
+    dispatch(1 + second)
+
+    def far_piece(i, carry):
+        k = i % 2 * 2 + i // 2
+        landed(2, k)
+        project(3, k, gathered[2, :, cols(k)])
+        return carry
+
+    lax.fori_loop(0, 4, far_piece, 0)
+    dispatch(3)
+    receive(1)
+    receive(2)
+    receive(3)
     wo_copy.wait()
-    with jax.named_scope("attend"):
-        attend(3)
-        attend(2)
-        fetch(3)
-        output_half(3, 0, None)
-        sums["a"]().start()
-        output_half(3, 1, None)
-        sums["b"]().start()
-        attend(1)
-        fetch(2)
-        output_half(2, 1, None)
-        sums["r1"]().start()
-        sums["a"]().wait_recv()
-        output_half(2, 0, half_a)
-        sums["r0"]().start()
-        attend(0)
-        fetch(1)
-        output_half(1, 0, None)
-        sums["l0"]().start()
-        sums["b"]().wait_recv()
-        output_half(1, 1, half_b)
-        sums["l1"]().start()
-        fetch(0)
+    attend(3)
+    mask(2)
+    attend(2)
+    mask(1)
+    attend(1)
+    mask(0)
+    fetch(3)
+    output_half(3, 0, None)
+    sums["a"]().start()
+    output_half(3, 1, None)
+    sums["b"]().start()
+    attend(0)
+    fetch(2)
+    output_half(2, 1, None)
+    sums["r1"]().start()
+    fetch(1)
+    output_half(1, 0, None)
+    sums["l0"]().start()
+    sums["a"]().wait_recv()
+    output_half(2, 0, half_a)
+    sums["r0"]().start()
+    sums["b"]().wait_recv()
+    output_half(1, 1, half_b)
+    sums["l1"]().start()
+    fetch(0)
 
     def own_step(n, carry):
         at = tile(n)
-        own_part[:, at] = x_ref[:, at].astype(F32) + dot(unpacked[...], w_out[:, at])
+        own_part[:, at] = x_ref[:, at].astype(F32) + dot(unpacked[0], w_out[:, at])
         return carry
 
     lax.fori_loop(0, 2 * per_half, own_step, 0)
@@ -385,20 +442,29 @@
 
         lax.fori_loop(0, per_half, step, 0)
 
+    stores = [
+        pltpu.make_async_copy(out_ref.at[:, halves[i]], out_hbm.at[:, halves[i]], out_sem.at[i]) for i in range(2)
+    ]
     for which in range(2):
         sums[f"r{which}"]().wait_recv()
         sums[f"l{which}"]().wait_recv()
         finish(which)
+        stores[which].start()
 
     for k in range(4):
-        own_right(k).wait_send()
-        own_left(k).wait_send()
-        forward(k).wait_send()
+        own_ahead(k).wait_send()
+        to_partner(k).wait_send()
+        partner_ahead(k).wait_send()
+    for j in range(2):
+        forward(first, j, ahead).wait_send()
+        forward(second, j, behind).wait_send()
     for c in range(4):
         all_but_one(sent, c, send_sem)
         all_but_one(back_sent, c, back_send)
     for copy in sums.values():
         copy().wait_send()
+    for copy in stores:
+        copy.wait()
 
 
 def body(tokens, norm_gain, w_query, w_key, w_value, w_output, doc_lengths, pack_index):
@@ -412,17 +478,22 @@
     side = (per_kv + 2) * HEAD_DIM
     ctx = per_kv * HEAD_DIM
     chunk_slots = SLOTS * groups
-    index = jnp.swapaxes(pack_index.reshape(groups, members, rows), 0, 1)
-    vmem = pl.BlockSpec(memory_space=pltpu.VMEM)
+    index = pack_index.reshape(groups * members, rows)
     hbm = pl.BlockSpec(memory_space=pl.ANY)
     dma = pltpu.SemaphoreType.DMA
     V = pltpu.VMEM
     return pl.pallas_call(
         kernel,
         out_shape=jax.ShapeDtypeStruct((rows, width), BF16),
-        in_specs=[vmem, vmem, vmem, vmem, hbm, hbm, hbm, hbm],
-        out_specs=vmem,
+        in_specs=[hbm] * 8,
+        out_specs=hbm,
         scratch_shapes=[
+            V((rows, width), BF16),
+            V((1, width), F32),
+            V((groups * members, rows), jnp.int32),
+            V((1, doc_lengths.shape[0]), jnp.int32),
+            V((rows, width), BF16),
+            V((rows, width), BF16),
             V((width, total_cols), BF16),
             V(w_output.shape, BF16),
             V((3, rows, width), BF16),
@@ -430,9 +501,12 @@
             V((4, rows, total_cols), F32),
             V((4, rows, 128), F32),
             V((2 * rows, side), BF16),
+            V((4, rows, HEAD_DIM), F32),
+            V((4, rows, HEAD_DIM), F32),
+            V((4, 2 * SLOTS * groups, 2 * rows), BF16),
             V((4 * groups, 2 * SLOTS, side), BF16),
             V((4 * groups, 2 * SLOTS, side), BF16),
-            V((2, 4 * chunk_slots, side), BF16),
+            V((2, 4 * chunk_slots, side + HEAD_DIM), BF16),
             V((1, 4 * chunk_slots), F32),
             V((4, chunk_slots, 128), F32),
             V((4, chunk_slots, 128), F32),
@@ -441,15 +515,19 @@
             V((2, chunk_slots, ctx), BF16),
             V((4 * groups, 2 * SLOTS, ctx), BF16),
             V((4 * groups, 2 * SLOTS, ctx), BF16),
-            V((rows, 2 * ctx), BF16),
+            V((4, rows, 2 * ctx), BF16),
             V((3, rows, width), BF16),
             V((rows, width // 2), BF16),
             V((rows, width // 2), BF16),
             V((rows, width), BF16),
             V((rows, width), BF16),
             V((rows, width), F32),
+            dma((4,)),
+            dma((2,)),
             dma((3, 4)),
             dma,
+            dma((4,)),
+            dma((4,)),
             dma((3, 4)),
             dma((3, 4)),
             dma((4,)),

time: 132 us -> 113 us (0.86)
  Pallas kernels: 128 us -> 110 us
  local copies, waits for them, and re-layouts: 3.76 us -> 2.29 us
    pallas_call x1, Pallas kernels: 128 us -> 110 us  [body(): pl.pallas_call(kernel, out_shape=jax.ShapeDtypeStruct((rows, width), BF16...]
    reshape x1 -> x0, local copies, waits for them, and re-layouts: 1.47 us -> none  [body(): index = jnp.swapaxes(pack_index.reshape(groups, members, rows), 0, 1)]
where the time goes in v2:
time: 113 us; the launch traced here: 112 us
  Pallas kernels  110 us (97%)
  local copies, waits for them, and re-layouts  2.29 us (2%)
    pallas_call x1, Pallas kernels, body(): pl.pallas_call(kernel, out_shape=jax.ShapeDtypeStruct((rows, width), BF16...  110 us
    unnamed x1, local copies, waits for them, and re-layouts  2.29 us

profile of v2, /device:TPU:0, one launch (start us, length us, event | category | flops | bytes accessed | tf_op | source)
XLA Modules:
  0.0 112.0 jit_solution(4445775860959465981)
XLA Ops:
  0.0 109.7 %packed_attention.1 = bf16[128,4096]{1,0:T(8,128)(2,1)} custom-call(bf16[128,4096]{1,0:T(8,128)(2,1)} %x_hbm.1, f32[1,4096]{1,0:T(1,128)} %bitcast.4, s32[128,128]{1,0:T(8,128)} %bitcast.3, s32[1,128]{1,0:T(1,128)} %bitcast.5, bf16[4096,1024]{1,0:T(8,128)(2,1)} %wq_ref.1, bf16[4096,256]{1,0:T(8,128)(2,1)} %wk_ref.1, bf16[4096,256]{1,0:T(8,128)(2,1)} %wv_ref.1, ...), custom_call_target="tpu_custom_call" | custom-call | tf_op jit(solution)/shard_map/packed_attention/pallas_call | solution.py:485
  109.7 2.3 %copy.10 = bf16[128,4096]{1,0:T(8,128)(2,1)} copy(bf16[128,4096]{1,0:T(8,128)(2,1)} %packed_attention.1) | data formatting | bytes 2097152

commit v3 on v2

--- a/solution.py
+++ b/solution.py
@@ -24,11 +24,12 @@
 
 
 def kernel(
-    x_hbm, gain_hbm, pidx_hbm, len_hbm, wq_ref, wk_ref, wv_ref, wo_ref, out_hbm,
-    x_ref, gain_ref, pidx_ref, len_ref, partner_x, out_ref,
+    x_hbm, gain_hbm, pidx_hbm, len_hbm, wq_ref, wk_ref, wv_ref, wo_ref,
+    out_hbm,
+    x_ref, gain_ref, pidx_ref, len_ref, partner_x,
     w_all, w_out, gathered, scaled, acc, sumsq, stacked, cosines, sines, picks, sent, arrived, qkv,
     slot_row, slot_col, slot_start, bias, unpack, mixed, back_sent, back, unpacked,
-    part, half_a, half_b, from_left, from_right, own_part,
+    part, half_a, half_b, from_behind, from_ahead, own_part, early, early_peak,
     in_sem, out_sem, w_sem, wo_sem, pair_send, pair_recv, ag_send, ag_recv,
     send_sem, recv_sem, back_send, back_recv, rs_send, rs_recv,
 ):
@@ -45,10 +46,10 @@
     partner = me + 1 - 2 * core
     ahead = lax.rem(z + 1 + 2 * core, 4)
     behind = lax.rem(z + 3 - 2 * core, 4)
-    first, second = core, 1 - core
-
-    def member(c):
-        return lax.rem(z + c // 3 * 2 + (c % 3 + 1) // 2 * (1 + 2 * (c % 2)), 4)
+    own, first, second, far = 0, 1, 2, 3
+
+    def member(c, parity):
+        return lax.rem(z + (0, 3 - 2 * parity, 1 + 2 * parity, 2)[c], 4)
 
     q_cols = wq_ref.shape[1]
     k_cols = wk_ref.shape[1]
@@ -109,7 +110,7 @@
 
     def own_ahead(k):
         return copy_to(
-            x_ref.at[:, cols(k)], gathered.at[first, :, cols(k)], ag_send.at[0, k], ag_recv.at[first, k], (me, ahead)
+            x_ref.at[:, cols(k)], gathered.at[0, :, cols(k)], ag_send.at[0, k], ag_recv.at[0, k], (me, ahead)
         )
 
     def to_partner(k):
@@ -117,16 +118,16 @@
 
     def partner_ahead(k):
         return copy_to(
-            partner_x.at[:, cols(k)], gathered.at[first, :, cols(k)], ag_send.at[1, k], ag_recv.at[first, k], (partner, ahead)
+            partner_x.at[:, cols(k)], gathered.at[1, :, cols(k)], ag_send.at[1, k], ag_recv.at[1, k], (partner, ahead)
         )
 
-    def landed(slot, k):
-        piece_ref = gathered.at[slot, :, cols(k)]
-        pltpu.make_async_copy(piece_ref, piece_ref, ag_recv.at[slot, k]).wait()
-
-    def forward(slot, j, to):
-        k = 2 * slot + j
-        source = gathered.at[slot, :, cols(k)]
+    def landed(c, k):
+        piece_ref = gathered.at[c - 1, :, cols(k)]
+        pltpu.make_async_copy(piece_ref, piece_ref, ag_recv.at[c - 1, k]).wait()
+
+    def forward(k):
+        source = gathered.at[k // 2, :, cols(k)]
+        to = (ahead, behind)[k // 2]
         return copy_to(source, gathered.at[2, :, cols(k)], ag_send.at[2, k], ag_recv.at[2, k], (me, to))
 
     for k in range(4):
@@ -158,7 +159,11 @@
         return jnp.dot(a, b, preferred_element_type=F32)
 
     def slot_tables(c):
-        index = pidx_ref[pl.ds(member(c), groups, stride=4), :].astype(F32)
+        index = pidx_ref[pl.ds(member(c, 0), groups, stride=4), :]
+        if c in (first, second):
+            odd = iota((groups, rows), 0) % 2 == 1
+            index = jnp.where(odd, pidx_ref[pl.ds(member(c, 1), groups, stride=4), :], index)
+        index = index.astype(F32)
         mine = (index >= my_lo) & (index < my_hi)
         rank = dot(jnp.where(mine, 1.0, 0.0).astype(BF16), earlier)
         code = jnp.where(mine, rank, -1.0).astype(BF16)
@@ -182,21 +187,28 @@
     total_cols = q_cols + 2 * k_cols
     n_tile = 512
 
-    def project(c, k, x):
-        at = cols(k)
+    n_tiles = total_cols // n_tile
+
+    def scale_piece(c, k, slot, x):
         x = x.astype(F32)
         squares = sumsq[c]
         for j in range(piece // 128):
             block = x[:, j * 128 : (j + 1) * 128]
             squares = squares + block * block
         sumsq[c] = squares
-        scaled[...] = (x * gain_ref[:, at]).astype(BF16)
-        for n in range(total_cols // n_tile):
+        scaled[slot] = (x * gain_ref[:, cols(k)]).astype(BF16)
+
+    def multiply(c, k, slot, tiles):
+        for n in tiles:
             to = pl.ds(n * n_tile, n_tile)
-            acc[c, :, to] += dot(scaled[...], w_all[at, to])
+            acc[c, :, to] += dot(scaled[slot], w_all[cols(k), to])
+
+    def project(c, k, x):
+        scale_piece(c, k, 0, x)
+        multiply(c, k, 0, range(n_tiles))
 
     def prepare(c):
-        index = pidx_ref[pl.ds(4 * me + member(c), 1), :].astype(F32)
+        index = pidx_ref[pl.ds(4 * me + member(c, core), 1), :].astype(F32)
         eye = iota((rows, rows), 0) == iota((rows, rows), 1)
         index_col = jnp.sum(jnp.where(eye, index, 0.0), axis=1, keepdims=True)
         begin = jnp.max(jnp.where(starts_row <= index_col, starts_row, 0.0), axis=1, keepdims=True)
@@ -216,7 +228,11 @@
             unpack[c, pl.ds(g * rows, rows), :] = jnp.transpose(pick).astype(BF16)
             picks[c, :, pl.ds(g * rows, rows)] = pick.astype(BF16)
 
-    def dispatch(c):
+    query_lanes = pl.ds(0, ctx)
+    pair_lanes = pl.ds(ctx, 2 * HEAD_DIM)
+    all_lanes = pl.ds(0, side)
+
+    def rotate_pairs(c, kind):
         scale = lax.rsqrt(jnp.sum(sumsq[c], axis=1, keepdims=True) * (1.0 / width) + norm_eps)
         cosine = cosines[c]
         sine = sines[c]
@@ -230,24 +246,29 @@
 
         for g in range(kv_heads):
             at = pl.ds(g * rows, rows)
-            for j in range(per_kv):
-                stacked[at, pl.ds(j * HEAD_DIM, HEAD_DIM)] = rope(head(g * per_kv + j, query_scale)).astype(BF16)
-            stacked[at, pl.ds(ctx, HEAD_DIM)] = rope(head(heads + g, scale)).astype(BF16)
-            stacked[at, pl.ds(ctx + HEAD_DIM, HEAD_DIM)] = head(heads + kv_heads + g, scale).astype(BF16)
+            if kind != "pair":
+                for j in range(per_kv):
+                    stacked[at, pl.ds(j * HEAD_DIM, HEAD_DIM)] = rope(head(g * per_kv + j, query_scale)).astype(BF16)
+            if kind != "query":
+                stacked[at, pl.ds(ctx, HEAD_DIM)] = rope(head(heads + g, scale)).astype(BF16)
+                stacked[at, pl.ds(ctx + HEAD_DIM, HEAD_DIM)] = head(heads + kv_heads + g, scale).astype(BF16)
+
+    def dispatch(c, kind="all"):
+        lanes, sem = {"all": (all_lanes, c), "pair": (pair_lanes, c), "query": (query_lanes, 4)}[kind]
+        rotate_pairs(c, kind)
         for b in range(groups // nb):
             block = picks[c, pl.ds(b * nb * pack_rows, nb * pack_rows), :]
-            sent[pl.ds(c * groups + b * nb, nb)] = (
-                dot(block, stacked[...]).astype(BF16).reshape(nb, pack_rows, side)
-            )
-        arrived[c * groups + me] = sent[c * groups + me]
+            packed = dot(block, stacked[:, lanes]).astype(BF16)
+            sent[pl.ds(c * groups + b * nb, nb), :, lanes] = packed.reshape(nb, pack_rows, packed.shape[1])
+        arrived[c * groups + me, :, lanes] = sent[c * groups + me, :, lanes]
 
         def send(i, carry):
             to = lax.rem(me + i, groups)
             pltpu.make_async_remote_copy(
-                src_ref=sent.at[c * groups + to],
-                dst_ref=arrived.at[c * groups + me],
-                send_sem=send_sem.at[c],
-                recv_sem=recv_sem.at[c],
+                src_ref=sent.at[c * groups + to, :, lanes],
+                dst_ref=arrived.at[c * groups + me, :, lanes],
+                send_sem=send_sem.at[sem],
+                recv_sem=recv_sem.at[sem],
                 device_id=(to, z),
                 device_id_type=MESH,
             ).start()
@@ -255,9 +276,9 @@
 
         lax.fori_loop(1, groups, send, 0)
 
-    def all_but_one(ref, c, sem):
-        block = ref.at[pl.ds(c * groups, groups - 1)]
-        pltpu.make_async_copy(block, block, sem.at[c]).wait()
+    def all_but_one(ref, c, lanes, sem):
+        block = ref.at[pl.ds(c * groups, groups - 1), :, lanes]
+        pltpu.make_async_copy(block, block, sem).wait()
 
     reorder_rows = pack_rows * nb
     out_row = iota((reorder_rows, reorder_rows), 0)
@@ -268,13 +289,14 @@
     source_back = (in_row % split) // SLOTS * pack_rows + in_row // split * SLOTS + in_row % SLOTS
     together = (source_back == out_row).astype(BF16)
 
-    def receive(c):
-        all_but_one(arrived, c, recv_sem)
+    def receive(c, kind="all"):
+        lanes, sem = {"all": (all_lanes, c), "pair": (pair_lanes, c), "query": (query_lanes, 4)}[kind]
+        all_but_one(arrived, c, lanes, recv_sem.at[sem])
         for b in range(groups // nb):
-            block = arrived[pl.ds(c * groups + b * nb, nb)].reshape(reorder_rows, side)
-            ordered = dot(apart, block).astype(BF16)
+            block = arrived[pl.ds(c * groups + b * nb, nb), :, lanes]
+            ordered = dot(apart, block.reshape(reorder_rows, block.shape[2])).astype(BF16)
             for g in range(2):
-                qkv[g, pl.ds(c * chunk_slots + b * split, split), pl.ds(0, side)] = ordered[g * split : (g + 1) * split]
+                qkv[g, pl.ds(c * chunk_slots + b * split, split), lanes] = ordered[g * split : (g + 1) * split]
 
     def mask(c):
         found = slot_col[c][:, :1]
@@ -282,20 +304,41 @@
         keys = slot_row[...]
         bias[...] = jnp.where((keys >= begin) & (keys <= found), 0.0, score_floor)
 
-    def attend(c):
-        at = pl.ds(c * chunk_slots, chunk_slots)
-
+    early_keys = pl.ds(0, far * chunk_slots)
+    late_keys = pl.ds(far * chunk_slots, chunk_slots)
+    every_key = pl.ds(0, 4 * chunk_slots)
+
+    def scored(c, i, keys):
+        g = i // per_kv
+        query = qkv[g, pl.ds(c * chunk_slots, chunk_slots), pl.ds(i % per_kv * HEAD_DIM, HEAD_DIM)]
+        key = qkv[g, keys, pl.ds(ctx, HEAD_DIM)]
+        scores = lax.dot_general(query, key, (((1,), (1,)), ((), ())), preferred_element_type=F32)
+        scores = scores + bias[:, keys]
+        return scores, jnp.max(scores, axis=1, keepdims=True)
+
+    def weighted(i, scores, peak, keys):
+        weights = jnp.exp2(scores - peak).astype(BF16)
+        return dot(weights, qkv[i // per_kv, keys, pl.ds(ctx + HEAD_DIM, 2 * HEAD_DIM)])
+
+    def attend_early(c):
         for i in range(heads):
-            g = i // per_kv
-            lanes = pl.ds(i % per_kv * HEAD_DIM, HEAD_DIM)
-            query = qkv[g, at, lanes]
-            key = qkv[g, :, pl.ds(ctx, HEAD_DIM)]
-            value = qkv[g, :, pl.ds(ctx + HEAD_DIM, 2 * HEAD_DIM)]
-            scores = lax.dot_general(query, key, (((1,), (1,)), ((), ())), preferred_element_type=F32)
-            scores = scores + bias[...]
-            weights = jnp.exp2(scores - jnp.max(scores, axis=1, keepdims=True))
-            both = dot(weights.astype(BF16), value)
-            mixed[g, :, lanes] = (both[:, :HEAD_DIM] / both[:, HEAD_DIM:]).astype(BF16)
+            scores, peak = scored(c, i, early_keys)
+            early[i] = weighted(i, scores, peak, early_keys)
+            early_peak[i] = jnp.broadcast_to(peak, (chunk_slots, HEAD_DIM))
+
+    def attend(c, resumed=False):
+        for i in range(heads):
+            keys = late_keys if resumed else every_key
+            scores, peak = scored(c, i, keys)
+            if resumed:
+                before = early_peak[i][:, :1]
+                peak = jnp.maximum(peak, before)
+                both = early[i] * jnp.exp2(before - peak) + weighted(i, scores, peak, keys)
+            else:
+                both = weighted(i, scores, peak, keys)
+            mixed[i // per_kv, :, pl.ds(i % per_kv * HEAD_DIM, HEAD_DIM)] = (
+                both[:, :HEAD_DIM] / both[:, HEAD_DIM:]
+            ).astype(BF16)
         for b in range(groups // nb):
             block = mixed[:, pl.ds(b * split, split), :].reshape(reorder_rows, ctx)
             back_sent[pl.ds(c * groups + b * nb, nb)] = dot(together, block).astype(BF16).reshape(nb, pack_rows, ctx)
@@ -315,11 +358,11 @@
 
         lax.fori_loop(1, groups, send, 0)
 
-    o_tile = min(512, half)
+    o_tile = min(512, half // 2)
     per_half = half // o_tile
 
     def fetch(c):
-        all_but_one(back, c, back_recv)
+        all_but_one(back, c, query_lanes, back_recv.at[c])
         block = back[pl.ds(c * groups, groups)].reshape(pack_rows * groups, ctx)
         both = dot(unpack[c], block).astype(BF16)
         for g in range(2):
@@ -328,7 +371,7 @@
     def tile(n):
         return pl.ds(pl.multiple_of(n * o_tile, 128), o_tile)
 
-    def output_half(c, which, extra):
+    def output_part(c, which, extra, share=0, of=1):
         def step(n, carry):
             at = tile(which * per_half + n)
             value = dot(unpacked[c], w_out[:, at])
@@ -337,16 +380,21 @@
             part[c - 1, :, at] = value.astype(BF16)
             return carry
 
-        lax.fori_loop(0, per_half, step, 0)
+        lax.fori_loop(share * per_half // of, (share + 1) * per_half // of, step, 0)
 
     halves = (pl.ds(0, half), pl.ds(half, half))
+    low, high = halves
+    one, two, third, fourth = (pl.ds(i * (half // 2), half // 2) for i in range(4))
     sums = {
-        "a": lambda: column_copy(part.at[2, :, halves[0]], half_a, rs_send.at[0], rs_recv.at[0], right),
-        "b": lambda: column_copy(part.at[2, :, halves[1]], half_b, rs_send.at[1], rs_recv.at[1], left),
-        "r0": lambda: column_copy(part.at[1, :, halves[0]], from_left.at[:, halves[0]], rs_send.at[2], rs_recv.at[2], right),
-        "r1": lambda: column_copy(part.at[1, :, halves[1]], from_left.at[:, halves[1]], rs_send.at[3], rs_recv.at[3], right),
-        "l0": lambda: column_copy(part.at[0, :, halves[0]], from_right.at[:, halves[0]], rs_send.at[4], rs_recv.at[4], left),
-        "l1": lambda: column_copy(part.at[0, :, halves[1]], from_right.at[:, halves[1]], rs_send.at[5], rs_recv.at[5], left),
+        "far_low": lambda: column_copy(part.at[2, :, low], half_a, rs_send.at[0], rs_recv.at[0], ahead),
+        "far_high": lambda: column_copy(part.at[2, :, high], half_b, rs_send.at[1], rs_recv.at[1], behind),
+        "second_one": lambda: column_copy(part.at[1, :, one], from_behind.at[:, one], rs_send.at[2], rs_recv.at[2], ahead),
+        "second_two": lambda: column_copy(part.at[1, :, two], from_behind.at[:, two], rs_send.at[7], rs_recv.at[7], ahead),
+        "second_third": lambda: column_copy(part.at[1, :, third], from_behind.at[:, third], rs_send.at[3], rs_recv.at[3], ahead),
+        "second_fourth": lambda: column_copy(part.at[1, :, fourth], from_behind.at[:, fourth], rs_send.at[6], rs_recv.at[6], ahead),
+        "first_low": lambda: column_copy(part.at[0, :, low], from_ahead.at[:, low], rs_send.at[4], rs_recv.at[4], behind),
+        "first_third": lambda: column_copy(part.at[0, :, third], from_ahead.at[:, third], rs_send.at[5], rs_recv.at[5], behind),
+        "first_fourth": lambda: column_copy(part.at[0, :, fourth], from_ahead.at[:, fourth], rs_send.at[8], rs_recv.at[8], behind),
     }
 
     for k in range(4):
@@ -364,66 +412,81 @@
         slot_tables(c)
     for g in range(2):
         qkv[g, :, pl.ds(side, HEAD_DIM)] = jnp.ones((4 * chunk_slots, HEAD_DIM), BF16)
-    mask(3)
+    mask(second)
 
     def first_piece(k, carry):
         landed(first, k)
-        project(1 + first, k, gathered[first, :, cols(k)])
+        project(first, k, gathered[0, :, cols(k)])
         return carry
 
     lax.fori_loop(0, 4, first_piece, 0)
-    for j in range(2):
-        forward(first, j, ahead).start()
-    dispatch(1 + first)
-    receive(0)
+    for k in range(2):
+        forward(k).start()
+    dispatch(first)
+    receive(own)
 
     def second_piece(k, carry):
         landed(second, k)
-        project(1 + second, k, gathered[second, :, cols(k)])
+        project(second, k, gathered[1, :, cols(k)])
         return carry
 
     lax.fori_loop(0, 4, second_piece, 0)
-    for j in range(2):
-        forward(second, j, behind).start()
-    dispatch(1 + second)
+    for k in range(2, 4):
+        forward(k).start()
+    dispatch(second)
 
     def far_piece(i, carry):
-        k = i % 2 * 2 + i // 2
-        landed(2, k)
-        project(3, k, gathered[2, :, cols(k)])
+        landed(far, 2 * i)
+        project(far, 2 * i, gathered[2, :, cols(2 * i)])
         return carry
 
-    lax.fori_loop(0, 4, far_piece, 0)
-    dispatch(3)
-    receive(1)
-    receive(2)
-    receive(3)
+    lax.fori_loop(0, 2, far_piece, 0)
+    for i in range(2):
+        k = 2 * i + 1
+        landed(far, k)
+        scale_piece(far, k, i, gathered[2, :, cols(k)])
+        multiply(far, k, i, range(n_tiles - 1, n_tiles))
+    dispatch(far, "pair")
+    for i in range(2):
+        multiply(far, 2 * i + 1, i, range(n_tiles - 1))
+    dispatch(far, "query")
+    receive(first)
+    receive(second)
+    attend_early(second)
+    receive(far, "pair")
+    attend(second, True)
+    mask(far)
+    receive(far, "query")
+    attend(far)
+    mask(first)
     wo_copy.wait()
-    attend(3)
-    mask(2)
-    attend(2)
-    mask(1)
-    attend(1)
-    mask(0)
-    fetch(3)
-    output_half(3, 0, None)
-    sums["a"]().start()
-    output_half(3, 1, None)
-    sums["b"]().start()
-    attend(0)
-    fetch(2)
-    output_half(2, 1, None)
-    sums["r1"]().start()
-    fetch(1)
-    output_half(1, 0, None)
-    sums["l0"]().start()
-    sums["a"]().wait_recv()
-    output_half(2, 0, half_a)
-    sums["r0"]().start()
-    sums["b"]().wait_recv()
-    output_half(1, 1, half_b)
-    sums["l1"]().start()
-    fetch(0)
+    fetch(second)
+    output_part(second, 1, None, 0, 2)
+    sums["second_third"]().start()
+    output_part(second, 1, None, 1, 2)
+    sums["second_fourth"]().start()
+    attend(first)
+    mask(own)
+    fetch(far)
+    output_part(far, 0, None)
+    sums["far_low"]().start()
+    output_part(far, 1, None)
+    sums["far_high"]().start()
+    attend(own)
+    fetch(first)
+    output_part(first, 0, None)
+    sums["first_low"]().start()
+    sums["far_low"]().wait_recv()
+    output_part(second, 0, half_a, 0, 2)
+    sums["second_one"]().start()
+    output_part(second, 0, half_a, 1, 2)
+    sums["second_two"]().start()
+    sums["far_high"]().wait_recv()
+    output_part(first, 1, half_b, 0, 2)
+    sums["first_third"]().start()
+    output_part(first, 1, half_b, 1, 2)
+    sums["first_fourth"]().start()
+    fetch(own)
 
     def own_step(n, carry):
         at = tile(n)
@@ -432,35 +495,35 @@
 
     lax.fori_loop(0, 2 * per_half, own_step, 0)
 
-    def finish(which):
-        def step(n, carry):
-            at = tile(which * per_half + n)
-            out_ref[:, at] = (
-                own_part[:, at] + from_left[:, at].astype(F32) + from_right[:, at].astype(F32)
-            ).astype(BF16)
-            return carry
-
-        lax.fori_loop(0, per_half, step, 0)
-
-    stores = [
-        pltpu.make_async_copy(out_ref.at[:, halves[i]], out_hbm.at[:, halves[i]], out_sem.at[i]) for i in range(2)
-    ]
-    for which in range(2):
-        sums[f"r{which}"]().wait_recv()
-        sums[f"l{which}"]().wait_recv()
-        finish(which)
-        stores[which].start()
+    for k in range(4):
+        partner_ahead(k).wait_send()
+    out_ref = partner_x
+
+    def finish(at):
+        out_ref[:, at] = (own_part[:, at] + from_behind[:, at].astype(F32) + from_ahead[:, at].astype(F32)).astype(BF16)
+
+    quarters = (
+        (one, ("second_one", "first_low")),
+        (two, ("second_two",)),
+        (third, ("first_third", "second_third")),
+        (fourth, ("first_fourth", "second_fourth")),
+    )
+    stores = [pltpu.make_async_copy(out_ref.at[:, at], out_hbm.at[:, at], out_sem.at[i]) for i, (at, _) in enumerate(quarters)]
+    for i in range(4):
+        at, names = quarters[i]
+        for name in names:
+            sums[name]().wait_recv()
+        finish(at)
+        stores[i].start()
 
     for k in range(4):
         own_ahead(k).wait_send()
         to_partner(k).wait_send()
-        partner_ahead(k).wait_send()
-    for j in range(2):
-        forward(first, j, ahead).wait_send()
-        forward(second, j, behind).wait_send()
+        forward(k).wait_send()
     for c in range(4):
-        all_but_one(sent, c, send_sem)
-        all_but_one(back_sent, c, back_send)
+        all_but_one(sent, c, all_lanes if c < far else pair_lanes, send_sem.at[c])
+        all_but_one(back_sent, c, query_lanes, back_send.at[c])
+    all_but_one(sent, far, query_lanes, send_sem.at[4])
     for copy in sums.values():
         copy().wait_send()
     for copy in stores:
@@ -493,11 +556,10 @@
             V((groups * members, rows), jnp.int32),
             V((1, doc_lengths.shape[0]), jnp.int32),
             V((rows, width), BF16),
-            V((rows, width), BF16),
             V((width, total_cols), BF16),
             V(w_output.shape, BF16),
             V((3, rows, width), BF16),
-            V((rows, piece), BF16),
+            V((2, rows, piece), BF16),
             V((4, rows, total_cols), F32),
             V((4, rows, 128), F32),
             V((2 * rows, side), BF16),
@@ -522,20 +584,22 @@
             V((rows, width), BF16),
             V((rows, width), BF16),
             V((rows, width), F32),
+            V((q_cols // HEAD_DIM, chunk_slots, 2 * HEAD_DIM), F32),
+            V((q_cols // HEAD_DIM, chunk_slots, HEAD_DIM), F32),
             dma((4,)),
-            dma((2,)),
+            dma((4,)),
             dma((3, 4)),
             dma,
             dma((4,)),
             dma((4,)),
             dma((3, 4)),
             dma((3, 4)),
+            dma((5,)),
+            dma((5,)),
             dma((4,)),
             dma((4,)),
-            dma((4,)),
-            dma((4,)),
-            dma((6,)),
-            dma((6,)),
+            dma((9,)),
+            dma((9,)),
         ],
         compiler_params=pltpu.CompilerParams(
             collective_id=0, has_side_effects=True, vmem_limit_bytes=67043328

time: 113 us -> 109 us (0.965)
  Pallas kernels: 110 us -> 106 us
    pallas_call x1, Pallas kernels: 110 us -> 106 us  [body(): pl.pallas_call(kernel, out_shape=jax.ShapeDtypeStruct((rows, width), BF16...]
where the time goes in v3:
time: 109 us; the launch traced here: 108 us
  Pallas kernels  106 us (97%)
  local copies, waits for them, and re-layouts  2.29 us (2%)
    pallas_call x1, Pallas kernels, body(): pl.pallas_call(kernel, out_shape=jax.ShapeDtypeStruct((rows, width), BF16...  106 us
    unnamed x1, local copies, waits for them, and re-layouts  2.29 us

profile of v3, /device:TPU:0, one launch (start us, length us, event | category | flops | bytes accessed | tf_op | source)
XLA Modules:
  0.0 108.4 jit_solution(15281999961398457787)
XLA Ops:
  0.0 106.1 %packed_attention.1 = bf16[128,4096]{1,0:T(8,128)(2,1)} custom-call(bf16[128,4096]{1,0:T(8,128)(2,1)} %x_hbm.1, f32[1,4096]{1,0:T(1,128)} %bitcast.4, s32[128,128]{1,0:T(8,128)} %bitcast.3, s32[1,128]{1,0:T(1,128)} %bitcast.5, bf16[4096,1024]{1,0:T(8,128)(2,1)} %wq_ref.1, bf16[4096,256]{1,0:T(8,128)(2,1)} %wk_ref.1, bf16[4096,256]{1,0:T(8,128)(2,1)} %wv_ref.1, ...), custom_call_target="tpu_custom_call" | custom-call | tf_op jit(solution)/shard_map/packed_attention/pallas_call | solution.py:548
  106.1 2.3 %copy.10 = bf16[128,4096]{1,0:T(8,128)(2,1)} copy(bf16[128,4096]{1,0:T(8,128)(2,1)} %packed_attention.1) | data formatting | bytes 2097152

commit v4 on v3

--- a/solution.py
+++ b/solution.py
@@ -46,10 +46,10 @@
     partner = me + 1 - 2 * core
     ahead = lax.rem(z + 1 + 2 * core, 4)
     behind = lax.rem(z + 3 - 2 * core, 4)
-    own, first, second, far = 0, 1, 2, 3
+    own, first, far, second = 0, 1, 2, 3
 
     def member(c, parity):
-        return lax.rem(z + (0, 3 - 2 * parity, 1 + 2 * parity, 2)[c], 4)
+        return lax.rem(z + (0, 3 - 2 * parity, 2, 1 + 2 * parity)[c], 4)
 
     q_cols = wq_ref.shape[1]
     k_cols = wk_ref.shape[1]
@@ -59,6 +59,7 @@
     side = (per_kv + 2) * HEAD_DIM
     ctx = per_kv * HEAD_DIM
     pack_rows = 2 * SLOTS
+    stride = 11
     nb = min(16, groups)
     chunk_slots = SLOTS * groups
 
@@ -81,11 +82,7 @@
     ]
     for copy in loads:
         copy.start()
-    for k in range(4):
-        for copy in w_copies(k):
-            copy.start()
     wo_copy = pltpu.make_async_copy(wo_ref, w_out, wo_sem)
-    wo_copy.start()
 
     barrier = pltpu.get_barrier_semaphore()
 
@@ -98,6 +95,9 @@
     lax.fori_loop(1, groups, greet, 0)
     for copy in loads:
         copy.wait()
+    for k in range(4):
+        for copy in w_copies(k):
+            copy.start()
     pl.semaphore_wait(barrier, groups + 2)
 
     def copy_to(src, dst, send, recv, device):
@@ -118,7 +118,7 @@
 
     def partner_ahead(k):
         return copy_to(
-            partner_x.at[:, cols(k)], gathered.at[1, :, cols(k)], ag_send.at[1, k], ag_recv.at[1, k], (partner, ahead)
+            partner_x.at[:, cols(k)], gathered.at[2, :, cols(k)], ag_send.at[2, k], ag_recv.at[2, k], (partner, ahead)
         )
 
     def landed(c, k):
@@ -126,9 +126,9 @@
         pltpu.make_async_copy(piece_ref, piece_ref, ag_recv.at[c - 1, k]).wait()
 
     def forward(k):
-        source = gathered.at[k // 2, :, cols(k)]
-        to = (ahead, behind)[k // 2]
-        return copy_to(source, gathered.at[2, :, cols(k)], ag_send.at[2, k], ag_recv.at[2, k], (me, to))
+        return copy_to(
+            gathered.at[0, :, cols(k)], gathered.at[1, :, cols(k)], ag_send.at[1, k], ag_recv.at[1, k], (me, ahead)
+        )
 
     for k in range(4):
         own_ahead(k).start()
@@ -263,7 +263,7 @@
         arrived[c * groups + me, :, lanes] = sent[c * groups + me, :, lanes]
 
         def send(i, carry):
-            to = lax.rem(me + i, groups)
+            to = lax.rem(me + stride * i, groups)
             pltpu.make_async_remote_copy(
                 src_ref=sent.at[c * groups + to, :, lanes],
                 dst_ref=arrived.at[c * groups + me, :, lanes],
@@ -304,8 +304,8 @@
         keys = slot_row[...]
         bias[...] = jnp.where((keys >= begin) & (keys <= found), 0.0, score_floor)
 
-    early_keys = pl.ds(0, far * chunk_slots)
-    late_keys = pl.ds(far * chunk_slots, chunk_slots)
+    early_keys = pl.ds(0, second * chunk_slots)
+    late_keys = pl.ds(second * chunk_slots, chunk_slots)
     every_key = pl.ds(0, 4 * chunk_slots)
 
     def scored(c, i, keys):
@@ -345,7 +345,7 @@
         back[c * groups + me] = back_sent[c * groups + me]
 
         def send(i, carry):
-            to = lax.rem(me + i, groups)
+            to = lax.rem(me + stride * i, groups)
             pltpu.make_async_remote_copy(
                 src_ref=back_sent.at[c * groups + to],
                 dst_ref=back.at[c * groups + me],
@@ -358,8 +358,9 @@
 
         lax.fori_loop(1, groups, send, 0)
 
-    o_tile = min(512, half // 2)
-    per_half = half // o_tile
+    quarter = width // 4
+    o_tile = min(512, quarter)
+    per_quarter = quarter // o_tile
 
     def fetch(c):
         all_but_one(back, c, query_lanes, back_recv.at[c])
@@ -371,163 +372,141 @@
     def tile(n):
         return pl.ds(pl.multiple_of(n * o_tile, 128), o_tile)
 
-    def output_part(c, which, extra, share=0, of=1):
-        def step(n, carry):
-            at = tile(which * per_half + n)
+    def quarter_of(i):
+        return pl.ds(i * quarter, quarter)
+
+    def output_quarter(c, i, extra=None):
+        for n in range(per_quarter):
+            at = pl.ds(i * quarter + n * o_tile, o_tile)
             value = dot(unpacked[c], w_out[:, at])
             if extra is not None:
-                value = value + extra[:, tile(n)].astype(F32)
+                value = value + extra[:, pl.ds(i % 2 * quarter + n * o_tile, o_tile)].astype(F32)
             part[c - 1, :, at] = value.astype(BF16)
-            return carry
-
-        lax.fori_loop(share * per_half // of, (share + 1) * per_half // of, step, 0)
-
-    halves = (pl.ds(0, half), pl.ds(half, half))
-    low, high = halves
-    one, two, third, fourth = (pl.ds(i * (half // 2), half // 2) for i in range(4))
-    sums = {
-        "far_low": lambda: column_copy(part.at[2, :, low], half_a, rs_send.at[0], rs_recv.at[0], ahead),
-        "far_high": lambda: column_copy(part.at[2, :, high], half_b, rs_send.at[1], rs_recv.at[1], behind),
-        "second_one": lambda: column_copy(part.at[1, :, one], from_behind.at[:, one], rs_send.at[2], rs_recv.at[2], ahead),
-        "second_two": lambda: column_copy(part.at[1, :, two], from_behind.at[:, two], rs_send.at[7], rs_recv.at[7], ahead),
-        "second_third": lambda: column_copy(part.at[1, :, third], from_behind.at[:, third], rs_send.at[3], rs_recv.at[3], ahead),
-        "second_fourth": lambda: column_copy(part.at[1, :, fourth], from_behind.at[:, fourth], rs_send.at[6], rs_recv.at[6], ahead),
-        "first_low": lambda: column_copy(part.at[0, :, low], from_ahead.at[:, low], rs_send.at[4], rs_recv.at[4], behind),
-        "first_third": lambda: column_copy(part.at[0, :, third], from_ahead.at[:, third], rs_send.at[5], rs_recv.at[5], behind),
-        "first_fourth": lambda: column_copy(part.at[0, :, fourth], from_ahead.at[:, fourth], rs_send.at[8], rs_recv.at[8], behind),
-    }
+
+    def partial_sum(c, i):
+        at = quarter_of(i)
+        if c == far:
+            target, to = ((half_a, ahead), (half_b, behind))[i // 2]
+            place = quarter_of(i % 2)
+        else:
+            target, to = ((from_behind, ahead) if c == second else (from_ahead, behind))
+            place = at
+        return column_copy(
+            part.at[c - 1, :, at], target.at[:, place], rs_send.at[c - 1, i], rs_recv.at[c - 1, i], to
+        )
+
+    def output_send(c, i, extra=None):
+        output_quarter(c, i, extra)
+        partial_sum(c, i).start()
 
     for k in range(4):
         for copy in w_copies(k):
             copy.wait()
         project(0, k, x_ref[:, cols(k)])
+    wo_copy.start()
     prepare(0)
     dispatch(0)
-    for k in range(4):
-        to_partner(k).wait_recv()
-        partner_ahead(k).start()
     for c in range(1, 4):
         prepare(c)
     for c in range(4):
         slot_tables(c)
     for g in range(2):
         qkv[g, :, pl.ds(side, HEAD_DIM)] = jnp.ones((4 * chunk_slots, HEAD_DIM), BF16)
-    mask(second)
-
-    def first_piece(k, carry):
+    mask(far)
+
+    for k in range(4):
         landed(first, k)
+        forward(k).start()
         project(first, k, gathered[0, :, cols(k)])
-        return carry
-
-    lax.fori_loop(0, 4, first_piece, 0)
-    for k in range(2):
-        forward(k).start()
+    for k in range(4):
+        to_partner(k).wait_recv()
+        partner_ahead(k).start()
     dispatch(first)
     receive(own)
 
+    def far_piece(k, carry):
+        landed(far, k)
+        project(far, k, gathered[1, :, cols(k)])
+        return carry
+
+    lax.fori_loop(0, 4, far_piece, 0)
+    dispatch(far)
+    receive(first)
+
     def second_piece(k, carry):
         landed(second, k)
-        project(second, k, gathered[1, :, cols(k)])
+        project(second, k, gathered[2, :, cols(k)])
         return carry
 
-    lax.fori_loop(0, 4, second_piece, 0)
-    for k in range(2, 4):
-        forward(k).start()
-    dispatch(second)
-
-    def far_piece(i, carry):
-        landed(far, 2 * i)
-        project(far, 2 * i, gathered[2, :, cols(2 * i)])
+    lax.fori_loop(0, 3, second_piece, 0)
+    landed(second, 3)
+    scale_piece(second, 3, 0, gathered[2, :, cols(3)])
+    multiply(second, 3, 0, range(n_tiles - 1, n_tiles))
+    dispatch(second, "pair")
+    multiply(second, 3, 0, range(n_tiles - 1))
+    dispatch(second, "query")
+    receive(far)
+    attend_early(far)
+    receive(second, "pair")
+    attend(far, True)
+    mask(first)
+    attend(first)
+    receive(second, "query")
+    mask(second)
+    attend(second)
+    wo_copy.wait()
+    fetch(far)
+    for i in (0, 2, 1, 3):
+        output_send(far, i)
+    fetch(first)
+    for i in (0, 1):
+        output_send(first, i)
+    mask(own)
+    attend(own)
+    fetch(second)
+    for i in (2, 3):
+        output_send(second, i)
+    for i in (0, 1):
+        partial_sum(far, i).wait_recv()
+        output_send(second, i, half_a)
+        partial_sum(far, i + 2).wait_recv()
+        output_send(first, i + 2, half_b)
+    fetch(own)
+
+    def own_step(n, carry):
+        at = pl.ds(pl.multiple_of(n * o_tile, 128), o_tile)
+        own_part[:, at] = x_ref[:, at].astype(F32) + dot(unpacked[own], w_out[:, at])
         return carry
 
-    lax.fori_loop(0, 2, far_piece, 0)
-    for i in range(2):
-        k = 2 * i + 1
-        landed(far, k)
-        scale_piece(far, k, i, gathered[2, :, cols(k)])
-        multiply(far, k, i, range(n_tiles - 1, n_tiles))
-    dispatch(far, "pair")
-    for i in range(2):
-        multiply(far, 2 * i + 1, i, range(n_tiles - 1))
-    dispatch(far, "query")
-    receive(first)
-    receive(second)
-    attend_early(second)
-    receive(far, "pair")
-    attend(second, True)
-    mask(far)
-    receive(far, "query")
-    attend(far)
-    mask(first)
-    wo_copy.wait()
-    fetch(second)
-    output_part(second, 1, None, 0, 2)
-    sums["second_third"]().start()
-    output_part(second, 1, None, 1, 2)
-    sums["second_fourth"]().start()
-    attend(first)
-    mask(own)
-    fetch(far)
-    output_part(far, 0, None)
-    sums["far_low"]().start()
-    output_part(far, 1, None)
-    sums["far_high"]().start()
-    attend(own)
-    fetch(first)
-    output_part(first, 0, None)
-    sums["first_low"]().start()
-    sums["far_low"]().wait_recv()
-    output_part(second, 0, half_a, 0, 2)
-    sums["second_one"]().start()
-    output_part(second, 0, half_a, 1, 2)
-    sums["second_two"]().start()
-    sums["far_high"]().wait_recv()
-    output_part(first, 1, half_b, 0, 2)
-    sums["first_third"]().start()
-    output_part(first, 1, half_b, 1, 2)
-    sums["first_fourth"]().start()
-    fetch(own)
-
-    def own_step(n, carry):
-        at = tile(n)
-        own_part[:, at] = x_ref[:, at].astype(F32) + dot(unpacked[0], w_out[:, at])
-        return carry
-
-    lax.fori_loop(0, 2 * per_half, own_step, 0)
-
+    lax.fori_loop(0, 4 * per_quarter, own_step, 0)
     for k in range(4):
         partner_ahead(k).wait_send()
     out_ref = partner_x
 
-    def finish(at):
+    def store(i):
+        at = quarter_of(i)
+        return pltpu.make_async_copy(out_ref.at[:, at], out_hbm.at[:, at], out_sem.at[i])
+
+    for i in (0, 2, 1, 3):
+        at = quarter_of(i)
+        partial_sum(second, i).wait_recv()
+        partial_sum(first, i).wait_recv()
         out_ref[:, at] = (own_part[:, at] + from_behind[:, at].astype(F32) + from_ahead[:, at].astype(F32)).astype(BF16)
-
-    quarters = (
-        (one, ("second_one", "first_low")),
-        (two, ("second_two",)),
-        (third, ("first_third", "second_third")),
-        (fourth, ("first_fourth", "second_fourth")),
-    )
-    stores = [pltpu.make_async_copy(out_ref.at[:, at], out_hbm.at[:, at], out_sem.at[i]) for i, (at, _) in enumerate(quarters)]
-    for i in range(4):
-        at, names = quarters[i]
-        for name in names:
-            sums[name]().wait_recv()
-        finish(at)
-        stores[i].start()
+        store(i).start()
 
     for k in range(4):
         own_ahead(k).wait_send()
         to_partner(k).wait_send()
         forward(k).wait_send()
     for c in range(4):
-        all_but_one(sent, c, all_lanes if c < far else pair_lanes, send_sem.at[c])
+        all_but_one(sent, c, all_lanes if c < second else pair_lanes, send_sem.at[c])
         all_but_one(back_sent, c, query_lanes, back_send.at[c])
-    all_but_one(sent, far, query_lanes, send_sem.at[4])
-    for copy in sums.values():
-        copy().wait_send()
-    for copy in stores:
-        copy.wait()
+    all_but_one(sent, second, query_lanes, send_sem.at[4])
+    for c in (first, far, second):
+        for i in range(4):
+            partial_sum(c, i).wait_send()
+    for i in range(4):
+        store(i).wait()
 
 
 def body(tokens, norm_gain, w_query, w_key, w_value, w_output, doc_lengths, pack_index):
@@ -559,7 +538,7 @@
             V((width, total_cols), BF16),
             V(w_output.shape, BF16),
             V((3, rows, width), BF16),
-            V((2, rows, piece), BF16),
+            V((1, rows, piece), BF16),
             V((4, rows, total_cols), F32),
             V((4, rows, 128), F32),
             V((2 * rows, side), BF16),
@@ -598,8 +577,8 @@
             dma((5,)),
             dma((4,)),
             dma((4,)),
-            dma((9,)),
-            dma((9,)),
+            dma((3, 4)),
+            dma((3, 4)),
         ],
         compiler_params=pltpu.CompilerParams(
             collective_id=0, has_side_effects=True, vmem_limit_bytes=67043328

time: 109 us -> 106 us (0.972)
  Pallas kernels: 106 us -> 104 us
    pallas_call x1, Pallas kernels: 106 us -> 104 us  [body(): pl.pallas_call(kernel, out_shape=jax.ShapeDtypeStruct((rows, width), BF16...]
where the time goes in v4:
time: 106 us
  Pallas kernels  104 us (98%)
  local copies, waits for them, and re-layouts  2.29 us (2%)
    pallas_call x1, Pallas kernels, body(): pl.pallas_call(kernel, out_shape=jax.ShapeDtypeStruct((rows, width), BF16...  104 us
    unnamed x1, local copies, waits for them, and re-layouts  2.29 us

profile of v4, /device:TPU:0, one launch (start us, length us, event | category | flops | bytes accessed | tf_op | source)
XLA Modules:
  0.0 105.8 jit_solution(9235054786444515032)
XLA Ops:
  0.0 103.5 %packed_attention.1 = bf16[128,4096]{1,0:T(8,128)(2,1)} custom-call(bf16[128,4096]{1,0:T(8,128)(2,1)} %x_hbm.1, f32[1,4096]{1,0:T(1,128)} %bitcast.4, s32[128,128]{1,0:T(8,128)} %bitcast.3, s32[1,128]{1,0:T(1,128)} %bitcast.5, bf16[4096,1024]{1,0:T(8,128)(2,1)} %wq_ref.1, bf16[4096,256]{1,0:T(8,128)(2,1)} %wk_ref.1, bf16[4096,256]{1,0:T(8,128)(2,1)} %wv_ref.1, ...), custom_call_target="tpu_custom_call" | custom-call | tf_op jit(solution)/shard_map/packed_attention/pallas_call | solution.py:527
  103.5 2.3 %copy.10 = bf16[128,4096]{1,0:T(8,128)(2,1)} copy(bf16[128,4096]{1,0:T(8,128)(2,1)} %packed_attention.1) | data formatting | bytes 2097152

commit v5 on v4

--- a/solution.py
+++ b/solution.py
@@ -27,8 +27,9 @@
     x_hbm, gain_hbm, pidx_hbm, len_hbm, wq_ref, wk_ref, wv_ref, wo_ref,
     out_hbm,
     x_ref, gain_ref, pidx_ref, len_ref, partner_x,
-    w_all, w_out, gathered, scaled, acc, sumsq, stacked, cosines, sines, picks, sent, arrived, qkv,
-    slot_row, slot_col, slot_start, bias, unpack, mixed, back_sent, back, unpacked,
+    w_all, w_out, gathered, scaled, acc, sumsq, stacked, cosines, sines, picks, sent, arrived,
+    sent_pair, arrived_pair, sent_query, arrived_query, qkv,
+    slot_row, slot_col, slot_start, bias, unpack, mixed, back_sent, back, far_sent, far_back, unpacked,
     part, half_a, half_b, from_behind, from_ahead, own_part, early, early_peak,
     in_sem, out_sem, w_sem, wo_sem, pair_send, pair_recv, ag_send, ag_recv,
     send_sem, recv_sem, back_send, back_recv, rs_send, rs_recv,
@@ -253,31 +254,41 @@
                 stacked[at, pl.ds(ctx, HEAD_DIM)] = rope(head(heads + g, scale)).astype(BF16)
                 stacked[at, pl.ds(ctx + HEAD_DIM, HEAD_DIM)] = head(heads + kv_heads + g, scale).astype(BF16)
 
+    def wires(c, kind):
+        if kind == "pair":
+            return pair_lanes, sent_pair, arrived_pair, c
+        if kind == "query":
+            return query_lanes, sent_query, arrived_query, 4
+        at = pl.ds(c * groups, groups)
+        return all_lanes, sent.at[at], arrived.at[at], c
+
+    def scatter(source, target, send_at, recv_at):
+        def send(i, carry):
+            to = lax.rem(me + stride * i, groups)
+            pltpu.make_async_remote_copy(
+                src_ref=source.at[to],
+                dst_ref=target.at[me],
+                send_sem=send_at,
+                recv_sem=recv_at,
+                device_id=(to, z),
+                device_id_type=MESH,
+            ).start()
+            return carry
+
+        lax.fori_loop(1, groups, send, 0)
+
     def dispatch(c, kind="all"):
-        lanes, sem = {"all": (all_lanes, c), "pair": (pair_lanes, c), "query": (query_lanes, 4)}[kind]
+        lanes, source, target, sem = wires(c, kind)
         rotate_pairs(c, kind)
         for b in range(groups // nb):
             block = picks[c, pl.ds(b * nb * pack_rows, nb * pack_rows), :]
             packed = dot(block, stacked[:, lanes]).astype(BF16)
-            sent[pl.ds(c * groups + b * nb, nb), :, lanes] = packed.reshape(nb, pack_rows, packed.shape[1])
-        arrived[c * groups + me, :, lanes] = sent[c * groups + me, :, lanes]
-
-        def send(i, carry):
-            to = lax.rem(me + stride * i, groups)
-            pltpu.make_async_remote_copy(
-                src_ref=sent.at[c * groups + to, :, lanes],
-                dst_ref=arrived.at[c * groups + me, :, lanes],
-                send_sem=send_sem.at[sem],
-                recv_sem=recv_sem.at[sem],
-                device_id=(to, z),
-                device_id_type=MESH,
-            ).start()
-            return carry
-
-        lax.fori_loop(1, groups, send, 0)
-
-    def all_but_one(ref, c, lanes, sem):
-        block = ref.at[pl.ds(c * groups, groups - 1), :, lanes]
+            source[pl.ds(b * nb, nb)] = packed.reshape(nb, pack_rows, packed.shape[1])
+        target[me] = source[me]
+        scatter(source, target, send_sem.at[sem], recv_sem.at[sem])
+
+    def all_but_one(ref, sem):
+        block = ref.at[pl.ds(0, groups - 1)]
         pltpu.make_async_copy(block, block, sem).wait()
 
     reorder_rows = pack_rows * nb
@@ -290,10 +301,10 @@
     together = (source_back == out_row).astype(BF16)
 
     def receive(c, kind="all"):
-        lanes, sem = {"all": (all_lanes, c), "pair": (pair_lanes, c), "query": (query_lanes, 4)}[kind]
-        all_but_one(arrived, c, lanes, recv_sem.at[sem])
+        lanes, _, target, sem = wires(c, kind)
+        all_but_one(target, recv_sem.at[sem])
         for b in range(groups // nb):
-            block = arrived[pl.ds(c * groups + b * nb, nb), :, lanes]
+            block = target[pl.ds(b * nb, nb)]
             ordered = dot(apart, block.reshape(reorder_rows, block.shape[2])).astype(BF16)
             for g in range(2):
                 qkv[g, pl.ds(c * chunk_slots + b * split, split), lanes] = ordered[g * split : (g + 1) * split]
@@ -326,51 +337,51 @@
             early[i] = weighted(i, scores, peak, early_keys)
             early_peak[i] = jnp.broadcast_to(peak, (chunk_slots, HEAD_DIM))
 
+    share = ctx // 2
+
+    def returns(c):
+        if c == far:
+            return [(pl.ds(i * share, share), far_sent.at[i], far_back.at[i], (c, 4)[i]) for i in range(2)]
+        at = pl.ds((0, 1, None, 2)[c] * groups, groups)
+        return [(query_lanes, back_sent.at[at], back.at[at], c)]
+
+    def send_back(lanes, source, target, sem):
+        for b in range(groups // nb):
+            block = mixed[:, pl.ds(b * split, split), lanes]
+            block = dot(together, block.reshape(reorder_rows, block.shape[2])).astype(BF16)
+            source[pl.ds(b * nb, nb)] = block.reshape(nb, pack_rows, block.shape[1])
+        target[me] = source[me]
+        scatter(source, target, back_send.at[sem], back_recv.at[sem])
+
     def attend(c, resumed=False):
-        for i in range(heads):
-            keys = late_keys if resumed else every_key
-            scores, peak = scored(c, i, keys)
-            if resumed:
-                before = early_peak[i][:, :1]
-                peak = jnp.maximum(peak, before)
-                both = early[i] * jnp.exp2(before - peak) + weighted(i, scores, peak, keys)
-            else:
-                both = weighted(i, scores, peak, keys)
-            mixed[i // per_kv, :, pl.ds(i % per_kv * HEAD_DIM, HEAD_DIM)] = (
-                both[:, :HEAD_DIM] / both[:, HEAD_DIM:]
-            ).astype(BF16)
-        for b in range(groups // nb):
-            block = mixed[:, pl.ds(b * split, split), :].reshape(reorder_rows, ctx)
-            back_sent[pl.ds(c * groups + b * nb, nb)] = dot(together, block).astype(BF16).reshape(nb, pack_rows, ctx)
-        back[c * groups + me] = back_sent[c * groups + me]
-
-        def send(i, carry):
-            to = lax.rem(me + stride * i, groups)
-            pltpu.make_async_remote_copy(
-                src_ref=back_sent.at[c * groups + to],
-                dst_ref=back.at[c * groups + me],
-                send_sem=back_send.at[c],
-                recv_sem=back_recv.at[c],
-                device_id=(to, z),
-                device_id_type=MESH,
-            ).start()
-            return carry
-
-        lax.fori_loop(1, groups, send, 0)
+        wanted = returns(c)
+        for j in range(per_kv):
+            for g in range(kv_heads):
+                i = g * per_kv + j
+                keys = late_keys if resumed else every_key
+                scores, peak = scored(c, i, keys)
+                if resumed:
+                    before = early_peak[i][:, :1]
+                    peak = jnp.maximum(peak, before)
+                    both = early[i] * jnp.exp2(before - peak) + weighted(i, scores, peak, keys)
+                else:
+                    both = weighted(i, scores, peak, keys)
+                mixed[g, :, pl.ds(j * HEAD_DIM, HEAD_DIM)] = (both[:, :HEAD_DIM] / both[:, HEAD_DIM:]).astype(BF16)
+            if (j + 1) * len(wanted) % per_kv == 0:
+                send_back(*wanted[(j + 1) * len(wanted) // per_kv - 1])
 
     quarter = width // 4
     o_tile = min(512, quarter)
     per_quarter = quarter // o_tile
 
     def fetch(c):
-        all_but_one(back, c, query_lanes, back_recv.at[c])
-        block = back[pl.ds(c * groups, groups)].reshape(pack_rows * groups, ctx)
-        both = dot(unpack[c], block).astype(BF16)
-        for g in range(2):
-            unpacked[c, :, pl.ds(g * ctx, ctx)] = both[g * rows : (g + 1) * rows]
-
-    def tile(n):
-        return pl.ds(pl.multiple_of(n * o_tile, 128), o_tile)
+        for lanes, _, target, sem in returns(c):
+            all_but_one(target, back_recv.at[sem])
+            block = target[...]
+            both = dot(unpack[c], block.reshape(pack_rows * groups, block.shape[2])).astype(BF16)
+            for g in range(2):
+                at = pl.ds(g * ctx + lanes.start, lanes.size)
+                unpacked[c, :, at] = both[g * rows : (g + 1) * rows]
 
     def quarter_of(i):
         return pl.ds(i * quarter, quarter)
@@ -414,10 +425,13 @@
         qkv[g, :, pl.ds(side, HEAD_DIM)] = jnp.ones((4 * chunk_slots, HEAD_DIM), BF16)
     mask(far)
 
-    for k in range(4):
+    def first_piece(k, carry):
         landed(first, k)
         forward(k).start()
         project(first, k, gathered[0, :, cols(k)])
+        return carry
+
+    lax.fori_loop(0, 4, first_piece, 0)
     for k in range(4):
         to_partner(k).wait_recv()
         partner_ahead(k).start()
@@ -453,11 +467,11 @@
     attend(first)
     receive(second, "query")
     mask(second)
-    attend(second)
     wo_copy.wait()
     fetch(far)
     for i in (0, 2, 1, 3):
         output_send(far, i)
+    attend(second)
     fetch(first)
     for i in (0, 1):
         output_send(first, i)
@@ -498,10 +512,12 @@
         own_ahead(k).wait_send()
         to_partner(k).wait_send()
         forward(k).wait_send()
+    for c, kind in ((own, "all"), (first, "all"), (far, "all"), (second, "pair"), (second, "query")):
+        _, source, _, sem = wires(c, kind)
+        all_but_one(source, send_sem.at[sem])
     for c in range(4):
-        all_but_one(sent, c, all_lanes if c < second else pair_lanes, send_sem.at[c])
-        all_but_one(back_sent, c, query_lanes, back_send.at[c])
-    all_but_one(sent, second, query_lanes, send_sem.at[4])
+        for _, source, _, sem in returns(c):
+            all_but_one(source, back_send.at[sem])
     for c in (first, far, second):
         for i in range(4):
             partial_sum(c, i).wait_send()
@@ -545,8 +561,12 @@
             V((4, rows, HEAD_DIM), F32),
             V((4, rows, HEAD_DIM), F32),
             V((4, 2 * SLOTS * groups, 2 * rows), BF16),
-            V((4 * groups, 2 * SLOTS, side), BF16),
-            V((4 * groups, 2 * SLOTS, side), BF16),
+            V((3 * groups, 2 * SLOTS, side), BF16),
+            V((3 * groups, 2 * SLOTS, side), BF16),
+            V((groups, 2 * SLOTS, 2 * HEAD_DIM), BF16),
+            V((groups, 2 * SLOTS, 2 * HEAD_DIM), BF16),
+            V((groups, 2 * SLOTS, ctx), BF16),
+            V((groups, 2 * SLOTS, ctx), BF16),
             V((2, 4 * chunk_slots, side + HEAD_DIM), BF16),
             V((1, 4 * chunk_slots), F32),
             V((4, chunk_slots, 128), F32),
@@ -554,8 +574,10 @@
             V((chunk_slots, 4 * chunk_slots), F32),
             V((4, 2 * rows, 2 * SLOTS * groups), BF16),
             V((2, chunk_slots, ctx), BF16),
-            V((4 * groups, 2 * SLOTS, ctx), BF16),
-            V((4 * groups, 2 * SLOTS, ctx), BF16),
+            V((3 * groups, 2 * SLOTS, ctx), BF16),
+            V((3 * groups, 2 * SLOTS, ctx), BF16),
+            V((2, groups, 2 * SLOTS, ctx // 2), BF16),
+            V((2, groups, 2 * SLOTS, ctx // 2), BF16),
             V((4, rows, 2 * ctx), BF16),
             V((3, rows, width), BF16),
             V((rows, width // 2), BF16),
@@ -575,8 +597,8 @@
             dma((3, 4)),
             dma((5,)),
             dma((5,)),
-            dma((4,)),
-            dma((4,)),
+            dma((5,)),
+            dma((5,)),
             dma((3, 4)),
             dma((3, 4)),
         ],

time: 106 us -> 103 us (0.972)
  Pallas kernels: 104 us -> 100 us
    pallas_call x1, Pallas kernels: 104 us -> 100 us  [body(): pl.pallas_call(kernel, out_shape=jax.ShapeDtypeStruct((rows, width), BF16...]
where the time goes in v5:
time: 103 us
  Pallas kernels  100 us (97%)
  local copies, waits for them, and re-layouts  2.29 us (2%)
    pallas_call x1, Pallas kernels, body(): pl.pallas_call(kernel, out_shape=jax.ShapeDtypeStruct((rows, width), BF16...  100 us
    unnamed x1, local copies, waits for them, and re-layouts  2.29 us

profile of v5, /device:TPU:0, one launch (start us, length us, event | category | flops | bytes accessed | tf_op | source)
XLA Modules:
  0.0 102.8 jit_solution(7107808351182682174)
XLA Ops:
  0.0 100.5 %packed_attention.1 = bf16[128,4096]{1,0:T(8,128)(2,1)} custom-call(bf16[128,4096]{1,0:T(8,128)(2,1)} %x_hbm.1, f32[1,4096]{1,0:T(1,128)} %bitcast.4, s32[128,128]{1,0:T(8,128)} %bitcast.3, s32[1,128]{1,0:T(1,128)} %bitcast.5, bf16[4096,1024]{1,0:T(8,128)(2,1)} %wq_ref.1, bf16[4096,256]{1,0:T(8,128)(2,1)} %wk_ref.1, bf16[4096,256]{1,0:T(8,128)(2,1)} %wv_ref.1, ...), custom_call_target="tpu_custom_call" | custom-call | tf_op jit(solution)/shard_map/packed_attention/pallas_call | solution.py:543
  100.5 2.3 %copy.10 = bf16[128,4096]{1,0:T(8,128)(2,1)} copy(bf16[128,4096]{1,0:T(8,128)(2,1)} %packed_attention.1) | data formatting | bytes 2097152
